TPU v7x, 128 devices: a whole 4x4x4 slice. The times are simulated.
128 devices in a mesh: dp: 4 (over x), fsdp: 8 (over y, core), enc: 4 (over z).
Axes of the slice: x: 4, y: 4, z: 4, core: 2. Of those that a mesh axis runs over, the one named last changes fastest.
Arguments:
- hidden: bfloat16 [32768, 8192], P(('dp', 'fsdp', 'enc')), may hold values from -40 to 40
- residual_gradient: bfloat16 [32768, 8192], P(('dp', 'fsdp', 'enc')), may hold values from -3 to 3
- value_output_gradient: bfloat16 [32768, 1024], P(('dp', 'fsdp', 'enc')), may hold values from -6 to 6
- attention_norm_gain: float32 [8192], replicated, may hold values from 0.1 to 1.9
- value_frozen_weight: bfloat16 [8192, 1024], P('fsdp'), may hold values from -0.0625 to 0.0625
- value_down_factor: bfloat16 [8192, 16], replicated, may hold values from -0.0625 to 0.0625
- value_up_factor: bfloat16 [16, 1024], replicated, may hold values from -0.29882812 to 0.29882812
- merger_frozen_weight: bfloat16 [5120, 8192], P(None, ('fsdp', 'enc')), may hold values from -0.078125 to 0.078125
- merger_down_factor: bfloat16 [5120, 16], replicated, may hold values from -0.078125 to 0.078125
- merger_up_factor: bfloat16 [16, 8192], P(None, ('fsdp', 'enc')), may hold values from -0.29882812 to 0.29882812
- merger_saved_preactivation: bfloat16 [4096, 5120], P(('dp', 'fsdp', 'enc')), may hold values from -5 to 5
- image_token_counts: int32 [128], P('dp'), may hold values from 8 to 16, as said below
- image_encoder_owner: int32 [128], P('dp'), may hold values from 0 to 31, as said below
- image_first_rows: int32 [128], P(('dp', 'fsdp', 'enc')), may hold values from 0 to 255, as said below
Outputs:
- layer_input_gradient: bfloat16 [32768, 8192], P(('dp', 'fsdp', 'enc'))
- preactivation_gradient: bfloat16 [4096, 5120], P(('dp', 'fsdp', 'enc'))
- value_down_gradient: float32 [8192, 16], replicated
- value_up_gradient: float32 [16, 1024], replicated
- merger_down_gradient: float32 [5120, 16], replicated
- merger_up_gradient: float32 [16, 8192], P(None, ('fsdp', 'enc'))
Inputs may be any that keep to these rules, and one draw needn't show every extreme that they name: `image_token_counts`: within each data replica some encoder device owns exactly 2 images, all of 16 visual tokens, so its rows fill all 32; no other device owns more than 2 images. `image_encoder_owner`: encoder devices are numbered within the data replica in mesh order. `image_first_rows`: images of one device lie inside its 256 rows in increasing order and don't intersect.
All inputs are finite; a program needn't handle non-finite values.
Results may differ from a plain program's by a relative error of at most 0.0085.
Values may be sent and summed in bfloat16 or wider, within the bound.
A program may use at most 192 MiB of HBM per device.

v0:
```python
import jax
import jax.numpy as jnp
from jax import lax
from jax.sharding import PartitionSpec as P

MAXIMG = 16


adapter_scale = 2.0
norm_eps = 1e-06


def laid_out(blocks, dim):
    shape = list(blocks.shape[1:])
    shape[dim] *= blocks.shape[0]
    return jnp.moveaxis(blocks, 0, dim).reshape(shape)


def sent_to_all(value, axis):
    copies = jnp.broadcast_to(value, (lax.axis_size(axis), *value.shape))
    return lax.all_to_all(copies, axis, split_axis=0, concat_axis=0, tiled=True)


def gathered_copies(value, axis, dim):
    return laid_out(sent_to_all(value, axis), dim)


def in_one_piece(arrays, axis, dim, along):
    widths = [a.shape[along] for a in arrays]
    both = jnp.concatenate(arrays, axis=along)
    out = lax.psum_scatter(both, axis, scatter_dimension=dim, tiled=True)
    return tuple(jnp.split(out, [sum(widths[:k]) for k in range(1, len(widths))], axis=along))


def over_copies(value, axis):
    return sent_to_all(value, axis).sum(axis=0)


def gelu_parts(preact):
    normal_cdf = 0.5 * (1.0 + lax.erf(preact * 0.7071067811865476))
    normal_pdf = jnp.exp(-0.5 * preact * preact) * 0.3989422804014327
    return (normal_cdf, normal_pdf)


def owner_layout(image_token_counts, image_encoder_owner, owner_count, owner_room, slot_len):
    total_images = image_token_counts.shape[0]
    image_ids = jnp.arange(total_images)
    same_owner = image_encoder_owner[:, None] == image_encoder_owner[None, :]
    earlier = image_ids[None, :] < image_ids[:, None]
    starts = jnp.sum(jnp.where(same_owner & earlier, image_token_counts[None, :], 0), axis=1)
    row_index = jnp.arange(owner_count * owner_room)
    row_owner = row_index // owner_room
    row_place = row_index % owner_room
    matches = (
        (row_owner[:, None] == image_encoder_owner[None, :])
        & (row_place[:, None] >= starts[None, :])
        & (row_place[:, None] < (starts + image_token_counts)[None, :])
    )
    source = jnp.sum(
        jnp.where(matches, image_ids[None, :] * slot_len + row_place[:, None] - starts[None, :], 0),
        axis=1,
    )
    valid_rows = jnp.any(matches, axis=1)
    return (source, valid_rows)


def take_slots(layer_input_gradient, counts_in, offsets_in):
    padded = jnp.concatenate(
        [
            layer_input_gradient,
            jnp.zeros((MAXIMG, layer_input_gradient.shape[1]), layer_input_gradient.dtype),
        ],
        axis=0,
    )
    window = lax.dynamic_slice_in_dim(padded, offsets_in[0], MAXIMG, 0)
    inside = jnp.arange(MAXIMG) < counts_in[0]
    pieces = jnp.where(inside[:, None], window, jnp.zeros_like(window))
    return pieces


def decoder_layer_block(
    incoming_rows,
    residual_input,
    value_incoming,
    attention_norm_gain,
    passed_gradient,
    value_down_factor,
    value_up_factor,
):
    values = incoming_rows.astype(jnp.float32)
    inverse = lax.rsqrt(jnp.mean(values * values, axis=1, keepdims=True) + norm_eps)
    normalized_input = (values * inverse * attention_norm_gain).astype(jnp.bfloat16)
    value_low_product = jnp.dot(
        value_incoming, value_up_factor.T, preferred_element_type=jnp.float32
    ).astype(jnp.bfloat16)
    normalized_gradient = passed_gradient.astype(jnp.float32) + adapter_scale * jnp.dot(
        value_low_product, value_down_factor.T, preferred_element_type=jnp.float32
    )
    gained = attention_norm_gain * normalized_gradient
    layer_input_gradient = (
        residual_input.astype(jnp.float32)
        + inverse * gained
        - values * inverse**3 * jnp.mean(values * gained, axis=1, keepdims=True)
    ).astype(jnp.bfloat16)
    projected_rows = jnp.dot(
        normalized_input, value_down_factor, preferred_element_type=jnp.float32
    ).astype(jnp.bfloat16)
    up_term = lax.dot_general(
        projected_rows, value_incoming, (((0,), (0,)), ((), ())), preferred_element_type=jnp.float32
    )
    down_term = lax.dot_general(
        normalized_input,
        value_low_product,
        (((0,), (0,)), ((), ())),
        preferred_element_type=jnp.float32,
    )
    return (layer_input_gradient, down_term, up_term)


def body(
    hidden,
    residual_gradient,
    value_output_gradient,
    attention_norm_gain,
    value_frozen_weight,
    value_down_factor,
    value_up_factor,
    merger_frozen_weight,
    merger_down_factor,
    merger_up_factor,
    merger_saved_preactivation,
    image_token_counts,
    image_encoder_owner,
    image_first_rows,
):
    device_total = lax.axis_size("dp") * lax.axis_size("fsdp") * lax.axis_size("enc")
    gradient_scale = 256.0 / (hidden.shape[0] * device_total)
    scale_factor = gradient_scale * adapter_scale
    owner_count = lax.axis_size("fsdp") * lax.axis_size("enc")
    owner_room = merger_saved_preactivation.shape[0]
    preact = merger_saved_preactivation.astype(jnp.float32)
    normal_cdf, normal_pdf = gelu_parts(preact)
    activation = (preact * normal_cdf).astype(jnp.bfloat16)
    act_low = jnp.dot(activation, merger_down_factor, preferred_element_type=jnp.float32).astype(
        jnp.bfloat16
    )
    all_low = gathered_copies(act_low, ("fsdp", "enc"), 0)
    columns = lax.dot_general(
        lax.all_gather(value_output_gradient, "fsdp", axis=0, tiled=True),
        value_frozen_weight,
        (((1,), (1,)), ((), ())),
        preferred_element_type=jnp.float32,
    ).astype(jnp.bfloat16)
    passed_gradient = lax.all_to_all(columns, "fsdp", split_axis=0, concat_axis=1, tiled=True)
    layer_input_gradient, down_term, up_term = decoder_layer_block(
        hidden,
        residual_gradient,
        value_output_gradient,
        attention_norm_gain,
        passed_gradient,
        value_down_factor,
        value_up_factor,
    )
    member = lax.axis_index(("fsdp", "enc"))
    local_images = image_first_rows.shape[0]
    local_counts = lax.dynamic_slice_in_dim(
        image_token_counts, member * local_images, local_images, 0
    )
    slots_out = take_slots(layer_input_gradient, local_counts, image_first_rows)
    received = lax.all_to_all(slots_out, ("fsdp", "enc"), split_axis=1, concat_axis=0, tiled=True)
    source, valid_rows = owner_layout(
        image_token_counts, image_encoder_owner, owner_count, owner_room, MAXIMG
    )
    visual_tokens = jnp.where(
        valid_rows[:, None], jnp.take(received, source, axis=0), jnp.zeros((), received.dtype)
    )
    value_partial_sum = lax.dot_general(
        visual_tokens,
        merger_frozen_weight,
        (((1,), (1,)), ((), ())),
        preferred_element_type=jnp.float32,
    )
    low_part = lax.dot_general(
        visual_tokens,
        merger_up_factor,
        (((1,), (1,)), ((), ())),
        preferred_element_type=jnp.float32,
    )
    value_partial_sum = value_partial_sum + adapter_scale * jnp.dot(
        low_part, merger_down_factor.astype(jnp.float32).T
    )
    combined_gradient, low_sum = in_one_piece((value_partial_sum, low_part), ("fsdp", "enc"), 0, 1)
    preactivation_gradient = (combined_gradient * (normal_cdf + preact * normal_pdf)).astype(
        jnp.bfloat16
    )
    term_a2 = lax.dot_general(
        activation,
        low_sum.astype(jnp.bfloat16),
        (((0,), (0,)), ((), ())),
        preferred_element_type=jnp.float32,
    )
    term_b2 = lax.dot_general(
        all_low, visual_tokens, (((0,), (0,)), ((), ())), preferred_element_type=jnp.float32
    )
    merger_up_gradient = over_copies(scale_factor * term_b2, "dp")
    value_down_gradient, value_up_gradient, merger_down_gradient = lax.psum(
        (scale_factor * down_term, scale_factor * up_term, scale_factor * term_a2),
        ("dp", "fsdp", "enc"),
    )
    return (
        layer_input_gradient,
        preactivation_gradient,
        value_down_gradient,
        value_up_gradient,
        merger_down_gradient,
        merger_up_gradient,
    )


def solution(mesh):
    placed = (
        P(("dp", "fsdp", "enc"), None),
        P(("dp", "fsdp", "enc"), None),
        P(("dp", "fsdp", "enc"), None),
        P(),
        P("fsdp", None),
        P(),
        P(),
        P(None, ("fsdp", "enc")),
        P(),
        P(None, ("fsdp", "enc")),
        P(("dp", "fsdp", "enc"), None),
        P("dp"),
        P("dp"),
        P(("dp", "fsdp", "enc")),
    )
    return jax.shard_map(
        body,
        mesh=mesh,
        in_specs=placed,
        out_specs=(
            P(("dp", "fsdp", "enc"), None),
            P(("dp", "fsdp", "enc"), None),
            P(),
            P(),
            P(),
            P(None, ("fsdp", "enc")),
        ),
        check_vma=False,
    )
```

profile of v0, /device:TPU:1, one launch (start us, length us, event | category | flops | bytes accessed | tf_op | source)
XLA Modules:
  0.0 477.0 jit_solution(13086993412335632943)
XLA Ops:
  7.2 0.0 all-gather.2.cloned.1.call-start
  7.2 0.7 all-gather.2.cloned.1.call-update
  7.9 37.5 %all-gather.2.cloned.1.call-done = bf16[2048,1024]{1,0:T(8,128)(2,1)} async-done(((bf16[256,1024]{1,0:T(8,128)(2,1)}), bf16[2048,1024]{1,0:T(8,128)(2,1)}) %all-gather.2.cloned.1.call-update) | async-done | bytes 4194320 | tf_op jit(solution)/shard_map/all_gather | solution.py:149
  45.4 9.4 %convolution_convert_fusion = bf16[2048,1024]{1,0:T(8,128)(2,1)} fusion(bf16[2048,1024]{1,0:T(8,128)(2,1)} %all-gather.2.cloned.1.call-done, bf16[1024,1024]{1,0:T(8,128)(2,1)} %param.18), kind=kOutput, calls=%fused_computation.21 | convolution fusion | flops 4297064448 | bytes 10485760 | tf_op jit(solution)/shard_map/dot_general | solution.py:148
  54.9 4.9 %all-to-all-start = ((bf16[8,256,1024]{2,1,0:T(8,128)(2,1)}), bf16[8,256,1024]{2,1,0:T(8,128)(2,1)}, u32[]{:S(2)}, u32[]{:S(2)}) async-start(bf16[8,256,1024]{2,1,0:T(8,128)(2,1)} %bitcast.44), calls=%async_computation | async-start | bytes 8388608 | tf_op jit(solution)/shard_map/all_to_all | solution.py:154
  60.4 0.6 dynamic_slice.6
  61.0 0.2 select_reduce_fusion.1
  61.2 0.7 iota_compare_fusion.1
  61.8 0.1 select_reduce_fusion
  62.0 0.2 convolution_convert_fusion.1
  62.2 46.3 %all-to-all-done = bf16[8,256,1024]{2,1,0:T(8,128)(2,1)} async-done(((bf16[8,256,1024]{2,1,0:T(8,128)(2,1)}), bf16[8,256,1024]{2,1,0:T(8,128)(2,1)}, u32[]{:S(2)}, u32[]{:S(2)}) %all-to-all-start) | async-done | bytes 4194336 | tf_op jit(solution)/shard_map/all_to_all | solution.py:154
  108.5 3.2 convert_bitcast_fusion
  111.8 1.7 copy.40
  113.4 4.9 %fusion.2 = (f32[256]{0:T(256)S(1)}, f32[256]{0:T(256)S(1)}, f32[256,8192]{1,0:T(8,128)S(1)}) fusion(bf16[256,8192]{1,0:T(8,128)(2,1)} %param.14, f32[256,8192]{1,0:T(8,128)S(1)} %bitcast.43, bf16[256,16]{0,1:T(8,128)(2,1)S(1)} %convolution_convert_fusion.1, bf16[8192,16]{0,1:T(8,128)(2,1)} %param.19, f32[8192]{0:T(1024)S(1)} %copy-done.8), kind=kOutput, calls=%fused_computation.11 | convolution fusion | flops 83885568 | bytes 21276672 | tf_op jit(solution)/shard_map/dot_general | solution.py:96
  118.4 3.4 fusion.5
  121.8 2.0 copy-done.3
  123.8 0.1 fusion.26
  124.0 0.7 copy.42
  124.7 6.1 %all-to-all-start.1 = ((bf16[16,32,256]{2,0,1:T(8,128)(2,1)}), bf16[16,32,256]{2,0,1:T(8,128)(2,1)S(1)}, u32[]{:S(2)}, u32[]{:S(2)}) async-start(bf16[16,32,256]{2,0,1:T(8,128)(2,1)} %bitcast.38), calls=%async_computation.1 | async-start | bytes 524288 | tf_op jit(solution)/shard_map/all_to_all | solution.py:170
  130.8 0.2 reduce-scatter.2.cloned.1.call-start
  131.1 0.1 fusion.35
  131.2 8.4 %all-to-all-done.1 = bf16[16,32,256]{2,0,1:T(8,128)(2,1)S(1)} async-done(((bf16[16,32,256]{2,0,1:T(8,128)(2,1)}), bf16[16,32,256]{2,0,1:T(8,128)(2,1)S(1)}, u32[]{:S(2)}, u32[]{:S(2)}) %all-to-all-start.1) | async-done | bytes 262176 | tf_op jit(solution)/shard_map/all_to_all | solution.py:170
  139.6 5.0 %gather_fusion = bf16[1024,256]{1,0:T(8,128)(2,1)} fusion(bf16[512,256]{1,0:T(8,128)(2,1)S(1)} %bitcast.42, s32[1024]{0:T(1024)S(1)} %broadcast_clamp_fusion), kind=kCustom, calls=%fused_computation | custom fusion | bytes 1052672 | tf_op jit(solution)/shard_map/jit(_take)/gather | solution.py:175
  144.6 1.4 select_select_fusion
  146.0 0.2 fusion.40
  146.2 8.6 %fusion.39 = f32[1024,5120]{1,0:T(8,128)} fusion(bf16[1024,256]{1,0:T(8,128)(2,1)S(1)} %select_select_fusion, bf16[5120,256]{1,0:T(8,128)(2,1)S(1)} %copy-done), kind=kOutput, calls=%fused_computation.73 | convolution fusion | flops 2684354560 | bytes 24117248 | tf_op jit(solution)/shard_map/dot_general | solution.py:177
  154.8 0.2 copy.37
  155.0 13.4 %multiply_add_fusion = f32[1024,5120]{1,0:T(8,128)} fusion(f32[1024,5120]{1,0:T(8,128)} %fusion.39, f32[1024,16]{0,1:T(8,128)S(1)} %fusion.40, bf16[5120,16]{0,1:T(8,128)(2,1)S(1)} %copy-done.7), kind=kOutput, calls=%fused_computation.2 | convolution fusion | flops 178257920 | bytes 42172416 | tf_op jit(solution)/shard_map/dot_general | solution.py:189
  168.4 15.5 %pad_maximum_fusion = f32[1024,5136]{1,0:T(8,128)} fusion(f32[1024,16]{1,0:T(8,128)S(1)} %copy.37, f32[1024,5120]{1,0:T(8,128)} %multiply_add_fusion), kind=kLoop, calls=%fused_computation.1 | loop fusion | flops 5259264 | bytes 42074112 | tf_op jit(solution)/shard_map/concatenate | solution.py:30
  183.9 0.0 reduce-scatter.2.cloned.1.call-update
  183.9 0.0 all-reduce.4.cloned.1.call-start
  184.0 4.3 convolution_multiply_fusion.1
  188.3 5.0 %convolution_multiply_fusion.3 = f32[16,1024]{1,0:T(8,128)} fusion(bf16[256,1024]{1,0:T(8,128)(2,1)} %param.16, bf16[8192,16]{0,1:T(8,128)(2,1)} %param.19, bf16[256,8192]{1,0:T(8,128)(2,1)} %param.14, f32[8192]{0:T(1024)S(1)} %copy-done.8, f32[256]{0:T(256)S(1)} %get-tuple-element.13), kind=kOutput, calls=%fused_computation.28 | convolution fusion | flops 83906560 | bytes 5080064 | tf_op jit(solution)/shard_map/dot_general | solution.py:108
  193.3 117.6 %reduce-scatter.2.cloned.1.call-done = f32[32,5136]{1,0:T(8,128)} async-done(((f32[1024,5136]{1,0:T(8,128)}), f32[32,5136]{1,0:T(8,128)}) %reduce-scatter.2.cloned.1.call-update) | async-done | bytes 657424 | tf_op jit(solution)/shard_map/reduce_scatter | solution.py:31
  310.8 2.1 fusion.24
  312.9 1.1 convolution_convert_fusion.2
  314.1 1.7 convolution_multiply_fusion.2
  315.8 0.1 reshape.107
  315.9 13.6 %all_to_all.42 = bf16[32,2,256]{2,1,0:T(2,128)(2,1)S(1)} all-to-all(bf16[32,2,256]{2,1,0:T(2,128)(2,1)S(1)} %reshape.107), channel_id=1, replica_groups=mesh['dp'=4,'fsdp'=8,'enc'=4] {'fsdp','enc'}, dimensions={0} | all-to-all | bytes 65536 | tf_op jit(solution)/shard_map/all_to_all | solution.py:21
  329.5 0.1 reshape.108
  329.7 0.2 reshape.97
  329.9 0.2 convolution_multiply_fusion.4
  330.1 8.2 %all_to_all.43 = f32[4,16,256]{2,1,0:T(8,128)S(1)} all-to-all(f32[4,16,256]{2,1,0:T(8,128)S(1)} %broadcast_in_dim.81), channel_id=1, replica_groups=mesh['dp'=4,'fsdp'=8,'enc'=4] {'dp'}, dimensions={0} | all-to-all | bytes 131072 | tf_op jit(solution)/shard_map/all_to_all | solution.py:21
  338.3 0.6 reduce_sum.52
  338.9 126.5 %all-reduce.4.cloned.1.call-done = (f32[8192,16]{0,1:T(8,128)}, f32[16,1024]{1,0:T(8,128)}, f32[5120,16]{0,1:T(8,128)}) async-done(((f32[8192,16]{0,1:T(8,128)}, f32[16,1024]{1,0:T(8,128)}, f32[5120,16]{0,1:T(8,128)}), (f32[8192,16]{0,1:T(8,128)}, f32[16,1024]{1,0:T(8,128)}, f32[5120,16]{0,1:T(8,128)})) %all-reduce.4.cloned.1.call-update) | async-done | bytes 917520 | tf_op jit(solution)/shard_map/psum | solution.py:206
  465.4 1.9 copy.47
  467.3 1.5 copy.48
  468.8 1.7 copy.49
  (36 shorter events, 0.2 us)
Async XLA Ops:
  7.2 139.1 %copy-start = (bf16[5120,256]{1,0:T(8,128)(2,1)S(1)}, bf16[5120,256]{1,0:T(8,128)(2,1)}, u32[]{:S(2)}) copy-start(bf16[5120,256]{1,0:T(8,128)(2,1)} %param.21) | copy-start | bytes 7864324
  7.2 38.2 %all-gather.2.cloned.1.call-start = ((), (), s32[]{:S(2)}) async-start(), calls=%async_computation.5 | async-start | bytes 4718592 | tf_op jit(solution)/shard_map/all_gather | solution.py:149
  54.8 5.5 %copy-start.12 = (s32[32]{0:T(128)S(1)}, s32[32]{0:T(128)}, u32[]{:S(2)}) copy-start(s32[32]{0:T(128)} %param.25) | copy-start | bytes 388
  54.8 6.1 %copy-start.11 = (s32[32]{0:T(128)S(1)}, s32[32]{0:T(128)}, u32[]{:S(2)}) copy-start(s32[32]{0:T(128)} %param.26) | copy-start | bytes 388
  54.9 7.1 %copy-start.6 = (bf16[256,1024]{1,0:T(8,128)(2,1)S(1)}, bf16[256,1024]{1,0:T(8,128)(2,1)}, u32[]{:S(2)}) copy-start(bf16[256,1024]{1,0:T(8,128)(2,1)} %param.16) | copy-start | bytes 1572868
  54.9 7.2 %copy-start.9 = (bf16[16,1024]{1,0:T(8,128)(2,1)S(1)}, bf16[16,1024]{1,0:T(8,128)(2,1)}, u32[]{:S(2)}) copy-start(bf16[16,1024]{1,0:T(8,128)(2,1)} %param.20) | copy-start | bytes 98308
  54.9 53.7 %all-to-all-start = ((bf16[8,256,1024]{2,1,0:T(8,128)(2,1)}), bf16[8,256,1024]{2,1,0:T(8,128)(2,1)}, u32[]{:S(2)}, u32[]{:S(2)}) async-start(bf16[8,256,1024]{2,1,0:T(8,128)(2,1)} %bitcast.44), calls=%async_computation | async-start | bytes 8388608 | tf_op jit(solution)/shard_map/all_to_all | solution.py:154
  111.7 1.7 copy-start.8
  113.4 5.0 %copy-start.2 = (bf16[256,8192]{1,0:T(8,128)(2,1)S(1)}, bf16[256,8192]{1,0:T(8,128)(2,1)}, u32[]{:S(2)}) copy-start(bf16[256,8192]{1,0:T(8,128)(2,1)} %param.14) | copy-start | bytes 12582916
  113.4 5.0 %copy-start.4 = (bf16[256,8192]{1,0:T(8,128)(2,1)S(1)}, bf16[256,8192]{1,0:T(8,128)(2,1)}, u32[]{:S(2)}) copy-start(bf16[256,8192]{1,0:T(8,128)(2,1)} %param.15) | copy-start | bytes 12582916
  121.8 2.0 copy-start.3
  123.8 22.1 %copy-start.10 = (bf16[16,256]{1,0:T(8,128)(2,1)S(1)}, bf16[16,256]{1,0:T(8,128)(2,1)}, u32[]{:S(2)}) copy-start(bf16[16,256]{1,0:T(8,128)(2,1)} %param.23) | copy-start | bytes 24580
  124.7 14.9 %all-to-all-start.1 = ((bf16[16,32,256]{2,0,1:T(8,128)(2,1)}), bf16[16,32,256]{2,0,1:T(8,128)(2,1)S(1)}, u32[]{:S(2)}, u32[]{:S(2)}) async-start(bf16[16,32,256]{2,0,1:T(8,128)(2,1)} %bitcast.38), calls=%async_computation.1 | async-start | bytes 524288 | tf_op jit(solution)/shard_map/all_to_all | solution.py:170
  130.8 180.0 %reduce-scatter.2.cloned.1.call-start = ((), (), s32[]{:S(2)}) async-start(), calls=%async_computation.6 | async-start | bytes 22167552 | tf_op jit(solution)/shard_map/reduce_scatter | solution.py:31
  146.2 8.8 %copy-start.7 = (bf16[5120,16]{0,1:T(8,128)(2,1)S(1)}, bf16[5120,16]{0,1:T(8,128)(2,1)}, u32[]{:S(2)}) copy-start(bf16[5120,16]{0,1:T(8,128)(2,1)} %param.22) | copy-start | bytes 491524
  183.9 126.9 %copy-start.5 = (bf16[32,5120]{1,0:T(8,128)(2,1)S(1)}, bf16[32,5120]{1,0:T(8,128)(2,1)}, u32[]{:S(2)}) copy-start(bf16[32,5120]{1,0:T(8,128)(2,1)} %param.24) | copy-start | bytes 983044
  183.9 281.5 %all-reduce.4.cloned.1.call-start = ((), (), s32[]{:S(2)}) async-start(), calls=%async_computation.7 | async-start | bytes 1835008 | tf_op jit(solution)/shard_map/psum | solution.py:206
  184.0 286.5 %copy-start.1 = (bf16[5120,256]{1,0:T(8,128)(2,1)S(1)}, bf16[5120,256]{1,0:T(8,128)(2,1)}, u32[]{:S(2)}) copy-start(bf16[5120,256]{1,0:T(8,128)(2,1)} %param.21) | copy-start | bytes 7864324
Sparse Core Ops, SparseCore 0:
  9.7 35.6 all-gather.1
  184.0 126.7 reduce-scatter.1
  316.7 148.6 all-reduce.3
where the time goes:
time: 478 us; the launch traced here: 477 us
  waiting for transfers between devices  337 us (71%)
  matrix products  49.1 us (10%)
  other arithmetic  27.4 us (6%)
  blocking collectives  21.8 us (5%)
  local copies, waits for them, and re-layouts  15.8 us (3%)
  between operations  14.7 us (3%)
  starting transfers between devices  11.3 us (2%)
    psum x1, waiting for transfers between devices, body(): lax.psum((scale_factor * down_term, scale_factor * up_term, scale_factor...  127 us
    reduce_scatter x1, waiting for transfers between devices, in_one_piece(): out = lax.psum_scatter(both, axis, scatter_dimension=dim, tiled=True)  118 us
    all_to_all x1, waiting for transfers between devices, body(): lax.all_to_all(columns, 'fsdp', split_axis=0, concat_axis=1, tiled=True)  46.3 us
    all_gather x1, waiting for transfers between devices, body(): lax.all_gather(value_output_gradient, 'fsdp', axis=0, tiled=True)  37.5 us
    all_to_all x2, blocking collectives, sent_to_all(): return lax.all_to_all(copies, axis, split_axis=0, concat_axis=0, tiled=True)  21.8 us
    concatenate x1, other arithmetic, in_one_piece(): both = jnp.concatenate(arrays, axis=along)  15.5 us
    dot_general x1, matrix products, body(): jnp.dot(low_part, merger_down_factor.astype(jnp.float32).T)  13.4 us
  transfers between devices with their start and end apart: 5, of which 5 were waited for; matrix products, arithmetic and copies ran while one was open for 3% of the time, Pallas kernels for 0%

commit v1 on v0

v1 whole, which is shorter than its diff:
```python
import functools

import jax
import jax.numpy as jnp
from jax import lax
from jax.experimental import pallas as pl
from jax.experimental.pallas import tpu as pltpu
from jax.sharding import PartitionSpec as P

MAXIMG = 16
adapter_scale = 2.0
norm_eps = 1e-06
F32, BF16 = jnp.float32, jnp.bfloat16
MESH = pl.DeviceIdType.MESH
VMEM = pl.BlockSpec(memory_space=pltpu.VMEM)
ANY = pl.BlockSpec(memory_space=pl.ANY)


def dot_nt(a, b):
    return lax.dot_general(a, b, (((1,), (1,)), ((), ())), preferred_element_type=F32)


def dot_tn(a, b):
    return lax.dot_general(a, b, (((0,), (0,)), ((), ())), preferred_element_type=F32)


def wrap(v, n):
    return lax.rem(v + n, n)


def place():
    f = lax.axis_index("fsdp")
    return lax.axis_index("dp"), f // 2, lax.axis_index("enc"), lax.rem(f, 2)


class Links:
    def __init__(self, send_sems, recv_sems):
        self.x, self.y, self.z, self.c = place()
        self.send_sems, self.recv_sems = send_sems, recv_sems
        self.made = []

    def peer(self, axis, step):
        if axis == "x":
            return {"dp": wrap(self.x + step, 4)}
        if axis == "z":
            return {"enc": wrap(self.z + step, 4)}
        if axis == "y":
            return {"fsdp": 2 * wrap(self.y + step, 4) + self.c}
        return {"fsdp": 2 * self.y + 1 - self.c}

    def send(self, axis, step, src, dst):
        k = len(self.made)
        copy = pltpu.make_async_remote_copy(
            src_ref=src,
            dst_ref=dst,
            send_sem=self.send_sems.at[k],
            recv_sem=self.recv_sems.at[k],
            device_id=self.peer(axis, step),
            device_id_type=MESH,
        )
        copy.start()
        self.made.append(copy)
        return copy

    def finish(self):
        for copy in self.made:
            copy.wait_send()

    def meet(self, peers):
        barrier = pltpu.get_barrier_semaphore()
        for axis, step in peers:
            pl.semaphore_signal(barrier, inc=1, device_id=self.peer(axis, step), device_id_type=MESH)
        pl.semaphore_wait(barrier, len(peers))


def image_kernel(
    vimg, ximg, rimg, keep, gain, wsh, up, down_t, act_low, wm, mup,
    vrecv, alow, wm_other, mup_other,
    vall, tout, timg, gained, visout,
    s1, r1, s2, r2, s3, r3, s4, r4, s5, r5, keep_sem,
):
    x, y, z, c = place()
    f = 2 * y + c
    me = f * 4 + z
    barrier = pltpu.get_barrier_semaphore()

    def greet(j, carry):
        d = lax.rem(me + j, 32)
        pl.semaphore_signal(
            barrier, inc=1, device_id={"fsdp": d // 4, "enc": lax.rem(d, 4)}, device_id_type=MESH
        )
        return carry

    lax.fori_loop(1, 32, greet, 0)
    pl.semaphore_wait(barrier, 31)

    def row(j, slot):
        return pltpu.make_async_remote_copy(
            src_ref=vimg, dst_ref=vall.at[slot], send_sem=s1.at[j], recv_sem=r1.at[j],
            device_id={"fsdp": lax.rem(f + j, 8)}, device_id_type=MESH,
        )

    def back(j, slot):
        return pltpu.make_async_remote_copy(
            src_ref=tout.at[lax.rem(f + j, 8)], dst_ref=timg.at[slot], send_sem=s2.at[j],
            recv_sem=r2.at[j], device_id={"fsdp": lax.rem(f + j, 8)}, device_id_type=MESH,
        )

    def spread(j, slot):
        d = lax.rem(me + j, 32)
        return pltpu.make_async_remote_copy(
            src_ref=visout.at[d // 8, lax.rem(d, 4)], dst_ref=vrecv.at[slot], send_sem=s3.at[j],
            recv_sem=r3.at[j], device_id={"fsdp": d // 4, "enc": lax.rem(d, 4)}, device_id_type=MESH,
        )

    def low_out(j, slot):
        d = lax.rem(me + j, 32)
        return pltpu.make_async_remote_copy(
            src_ref=act_low, dst_ref=alow.at[slot], send_sem=s4.at[j], recv_sem=r4.at[j],
            device_id={"fsdp": d // 4, "enc": lax.rem(d, 4)}, device_id_type=MESH,
        )

    def over(lo, hi, act):
        def step(j, carry):
            act(j)
            return carry

        lax.fori_loop(lo, hi, step, 0)

    over(1, 8, lambda j: row(j, f).start())
    wide = pltpu.make_async_remote_copy(
        src_ref=wm, dst_ref=wm_other, send_sem=s5.at[0], recv_sem=r5.at[0],
        device_id={"fsdp": 2 * y + 1 - c}, device_id_type=MESH,
    )
    thin = pltpu.make_async_remote_copy(
        src_ref=mup, dst_ref=mup_other, send_sem=s5.at[1], recv_sem=r5.at[1],
        device_id={"fsdp": 2 * y + 1 - c}, device_id_type=MESH,
    )
    wide.start()
    thin.start()
    over(1, 32, lambda j: low_out(j, me).start())
    alow[me] = act_low[...]
    vall[f] = vimg[...]
    low = dot_nt(vimg[...], up[...]).astype(BF16)
    over(1, 8, lambda j: row(j, lax.rem(f - j + 8, 8)).wait_recv())
    through = dot_nt(vall[...].reshape(128, 1024), wsh[...]).astype(BF16).reshape(8, 16, 1024)
    tout[...] = through
    over(1, 8, lambda j: back(j, f).start())
    timg[f] = tout[f]
    squares = jnp.zeros((16, 1), F32)
    for k in range(8):
        xs = ximg[:, k * 1024 : (k + 1) * 1024].astype(F32)
        squares = squares + jnp.sum(xs * xs, axis=1, keepdims=True)
    inverse = lax.rsqrt(squares * (1.0 / 8192) + norm_eps)
    over(1, 8, lambda j: back(j, lax.rem(f - j + 8, 8)).wait_recv())
    total = jnp.zeros((16, 1), F32)
    for k in range(8):
        cols = slice(k * 1024, (k + 1) * 1024)
        grad = timg[k].astype(F32) + adapter_scale * jnp.dot(
            low, down_t[k], preferred_element_type=F32
        )
        g = gain[k] * grad
        gained[k] = g
        total = total + jnp.sum(ximg[:, cols].astype(F32) * g, axis=1, keepdims=True)
    drop = inverse * inverse * inverse * (total * (1.0 / 8192))
    inside = keep[:, 0:1] > 0.5
    for k in range(8):
        cols = slice(k * 1024, (k + 1) * 1024)
        rows = rimg[:, cols].astype(F32) + inverse * gained[k] - ximg[:, cols].astype(F32) * drop
        rows = jnp.where(inside, rows, 0.0).astype(BF16)
        for b in range(4):
            visout[k // 2, b, k % 2] = rows[:, b * 256 : (b + 1) * 256]
    over(1, 32, lambda j: spread(j, me).start())
    vrecv[me] = visout[y, z]
    over(1, 32, lambda j: spread(j, lax.rem(me - j + 32, 32)).wait_recv())
    over(1, 32, lambda j: low_out(j, lax.rem(me - j + 32, 32)).wait_recv())
    wide.wait_recv()
    thin.wait_recv()
    over(1, 8, lambda j: row(j, f).wait_send())
    over(1, 8, lambda j: back(j, f).wait_send())
    over(1, 32, lambda j: spread(j, me).wait_send())
    over(1, 32, lambda j: low_out(j, me).wait_send())
    wide.wait_send()
    thin.wait_send()


def image_chain(vimg, ximg, rimg, keep, gain, wsh, up, down_t, act_low, wm, mup):
    dma = pltpu.SemaphoreType.DMA
    return pl.pallas_call(
        image_kernel,
        out_shape=(
            jax.ShapeDtypeStruct((32, 2, 16, 256), BF16),
            jax.ShapeDtypeStruct((32, 32, 128), BF16),
            jax.ShapeDtypeStruct(wm.shape, BF16),
            jax.ShapeDtypeStruct(mup.shape, BF16),
        ),
        in_specs=[VMEM] * 9 + [ANY, ANY],
        out_specs=(VMEM, VMEM, ANY, ANY),
        scratch_shapes=[
            pltpu.VMEM((8, 16, 1024), BF16),
            pltpu.VMEM((8, 16, 1024), BF16),
            pltpu.VMEM((8, 16, 1024), BF16),
            pltpu.VMEM((8, 16, 1024), F32),
            pltpu.VMEM((4, 4, 2, 16, 256), BF16),
            dma((8,)), dma((8,)), dma((8,)), dma((8,)),
            dma((32,)), dma((32,)), dma((32,)), dma((32,)),
            dma((2,)), dma((2,)), dma((1,)),
        ],
        compiler_params=pltpu.CompilerParams(collective_id=0, has_side_effects=True),
        name="image_chain",
    )(vimg, ximg, rimg, keep, gain, wsh, up, down_t, act_low, wm, mup)


def main_kernel(
    scale_factor,
    hidden, resid, wsh, v, up, gain, down_t,
    out, down_term, up_term,
    wbuf, xb, rb, gained, send_sems, recv_sems, local_sems, out_sems,
):
    links = Links(send_sems, recv_sems)
    x, y, z, c = links.x, links.y, links.z, links.c
    own = pltpu.make_async_copy(wsh, wbuf.at[c, 0], local_sems.at[0])
    own.start()
    loads = []
    for k in range(8):
        cols = pl.ds(k * 1024, 1024)
        a = pltpu.make_async_copy(hidden.at[:, cols], xb.at[k], local_sems.at[1 + k])
        b = pltpu.make_async_copy(resid.at[:, cols], rb.at[k], local_sems.at[9 + k])
        a.start()
        b.start()
        loads.append((a, b))
    links.meet([("x", 1), ("x", -1), ("y", 1), ("y", -1), ("z", 1), ("z", -1), ("c", 0)])
    own.wait()

    def rows(half, a, b, extra, count):
        at = ((half * 4 + a) * 4 + b) * 32 + extra
        return pl.ds(pl.multiple_of(at, 16), count)

    def at(j, span):
        return wbuf.at[c, j, span]

    inner = ((0, z, x), (1, x, z))
    first = ("x", "z")
    second = ("z", "x")

    def piece(half, step, extra, count):
        _, a, b = inner[half]
        return rows(half, a, wrap(b + step, 4), extra, count)

    def block(half, step, extra, count):
        _, a, _ = inner[half]
        return rows(half, wrap(a + step, 4), 0, extra, count)

    y1 = []
    for h in range(2):
        span = piece(h, 0, 0, 32)
        y1.append(
            (links.send("y", 1, at(0, span), at(3, span)), links.send("y", -1, at(0, span), at(1, span)))
        )
    across = {0: links.send("c", 0, wbuf.at[c, 0], wbuf.at[c, 0])}

    squares = jnp.zeros((256, 1), F32)
    for k in range(8):
        loads[k][0].wait()
        xs = xb[k].astype(F32)
        squares = squares + jnp.sum(xs * xs, axis=1, keepdims=True)
    inverse = lax.rsqrt(squares * (1.0 / 8192) + norm_eps)

    a1, a2, b1, b2 = {}, {}, {}, {}

    def start_a1(j):
        a1[j] = []
        for h in range(2):
            span = piece(h, 0, 0, 32)
            for step in (1, -1):
                a1[j].append(links.send(first[h], step, at(j, span), at(j, span)))

    def start_a2(j):
        a2[j] = []
        for h in range(2):
            for step, extra in ((1, 0), (-1, 16)):
                span = piece(h, -step, extra, 16)
                a2[j].append(links.send(first[h], step, at(j, span), at(j, span)))

    def start_b1(j):
        b1[j] = []
        for h in range(2):
            span = block(h, 0, 0, 128)
            for step in (1, -1):
                b1[j].append(links.send(second[h], step, at(j, span), at(j, span)))

    def start_b2(j):
        b2[j] = []
        for h in range(2):
            for step, extra in ((1, 0), (-1, 64)):
                span = block(h, -step, extra, 64)
                b2[j].append(links.send(second[h], step, at(j, span), at(j, span)))

    def arrived(copies):
        for copy in copies:
            copy.wait_recv()

    for pair in y1:
        arrived(pair)
    y2 = []
    for h in range(2):
        for step, j, extra in ((1, 3, 0), (-1, 1, 16)):
            span = piece(h, 0, extra, 16)
            y2.append(links.send("y", step, at(j, span), at(2, span)))
    start_a1(3)
    start_a1(1)

    low = dot_nt(v[...], up[...]).astype(BF16)
    low_t = dot_nt(up[...], v[...]).astype(BF16)
    arrived(y2)
    start_a1(2)

    projected_t = jnp.zeros((16, 256), F32)

    def normed_block(k, projected_t):
        normed = (xb[k].astype(F32) * inverse * gain[k]).astype(BF16)
        down_term[k] = scale_factor * jnp.dot(low_t, normed, preferred_element_type=F32)
        return projected_t + dot_nt(down_t[k], normed)

    def through_block(cs, j, total):
        k = 2 * lax.rem(y + j, 4) + cs
        through = dot_nt(v[...], wbuf[cs, j]).astype(BF16)
        grad = through.astype(F32) + adapter_scale * jnp.dot(
            low, down_t[k], preferred_element_type=F32
        )
        g = gain[k] * grad
        gained[k] = g
        return total + jnp.sum(xb[k].astype(F32) * g, axis=1, keepdims=True)

    total = jnp.zeros((256, 1), F32)
    order = (3, 1, 2)
    for n, j in enumerate(order):
        arrived(a1[j])
        start_a2(j)
        projected_t = normed_block(n, projected_t)
    for n, j in enumerate(order):
        arrived(a2[j])
        start_b1(j)
        projected_t = normed_block(3 + n, projected_t)
    projected_t = normed_block(6, projected_t)
    projected_t = normed_block(7, projected_t)
    up_term[...] = scale_factor * jnp.dot(
        projected_t.astype(BF16), v[...], preferred_element_type=F32
    )
    for n, j in enumerate(order):
        arrived(b1[j])
        start_b2(j)
        if n == 0:
            total = through_block(c, 0, total)
        if n == 1:
            across[0].wait_recv()
            total = through_block(1 - c, 0, total)
    last = None
    for j in order:
        arrived(b2[j])
        across[j] = links.send("c", 0, wbuf.at[c, j], wbuf.at[c, j])
        total = through_block(c, j, total)
        if last is not None:
            across[last].wait_recv()
            total = through_block(1 - c, last, total)
        last = j
    across[last].wait_recv()
    total = through_block(1 - c, last, total)

    drop = inverse * inverse * inverse * (total * (1.0 / 8192))
    stores = []
    for k in range(8):
        loads[k][1].wait()
        rows_out = rb[k].astype(F32) + inverse * gained[k] - xb[k].astype(F32) * drop
        rb[k] = rows_out.astype(BF16)
        store = pltpu.make_async_copy(rb.at[k], out.at[:, pl.ds(k * 1024, 1024)], out_sems.at[k])
        store.start()
        stores.append(store)
    for store in stores:
        store.wait()
    links.finish()


def main_block(scale_factor, hidden, resid, wsh, v, up, gain, down_t):
    dma = pltpu.SemaphoreType.DMA
    return pl.pallas_call(
        functools.partial(main_kernel, scale_factor),
        out_shape=(
            jax.ShapeDtypeStruct((256, 8192), BF16),
            jax.ShapeDtypeStruct((8, 16, 1024), F32),
            jax.ShapeDtypeStruct((16, 1024), F32),
        ),
        in_specs=[ANY, ANY, ANY, VMEM, VMEM, VMEM, VMEM],
        out_specs=(ANY, VMEM, VMEM),
        scratch_shapes=[
            pltpu.VMEM((2, 4, 1024, 1024), BF16),
            pltpu.VMEM((8, 256, 1024), BF16),
            pltpu.VMEM((8, 256, 1024), BF16),
            pltpu.VMEM((8, 256, 1024), F32),
            dma((64,)), dma((64,)), dma((17,)), dma((8,)),
        ],
        compiler_params=pltpu.CompilerParams(
            collective_id=1, has_side_effects=True, vmem_limit_bytes=60 * 1024 * 1024
        ),
        name="main_block",
    )(hidden, resid, wsh, v, up, gain, down_t)


def chunked(count, act):
    def step(i, carry):
        act(pl.ds(pl.multiple_of(i * 16, 16), 16))
        return carry

    lax.fori_loop(0, count // 16, step, 0)


class RingSum:
    def __init__(self, links, axis, blocks, relay, mid, near):
        self.links, self.axis, self.blocks = links, axis, blocks
        self.relay, self.mid, self.near = relay, mid, near
        m = links.x if axis == "x" else links.y if axis == "y" else links.z
        self.me, self.count = m, blocks.shape[2]

    def start(self):
        send, b, axis = self.links.send, self.blocks, self.axis
        far = wrap(self.me + 2, 4)
        right, left = wrap(self.me + 1, 4), wrap(self.me - 1, 4)
        self.far = [
            send(axis, 1, b.at[far, 0], self.relay.at[0]),
            send(axis, -1, b.at[far, 1], self.relay.at[1]),
        ]
        self.direct = [
            send(axis, 1, b.at[right, 1], self.near.at[0, 1]),
            send(axis, -1, b.at[left, 0], self.near.at[1, 0]),
        ]

    def forward(self):
        for way, step in ((0, 1), (1, -1)):
            self.far[way].wait_recv()
            to = wrap(self.me + step, 4)

            def add(span, way=way, to=to):
                self.mid[way, span] = (
                    self.blocks[to, way, span].astype(F32) + self.relay[way, span].astype(F32)
                ).astype(BF16)

            chunked(self.count, add)
            self.direct.append(
                self.links.send(self.axis, step, self.mid.at[way], self.near.at[way, way])
            )

    def finish(self, put):
        for copy in self.direct:
            copy.wait_recv()
        for half in range(2):

            def add(span, half=half):
                put(
                    half,
                    span,
                    self.blocks[self.me, half, span].astype(F32)
                    + self.near[0, half, span].astype(F32)
                    + self.near[1, half, span].astype(F32),
                )

            chunked(self.count, add)


def owner_kernel(
    qa, qb, outa, outb,
    relay_a, mid_a, near_a, next_a, relay_b, mid_b, near_b, next_b,
    relay_c, mid_c, near_c, relay_d, mid_d, near_d,
    send_sems, recv_sems,
):
    links = Links(send_sems, recv_sems)
    links.meet([("y", 1), ("y", -1), ("z", 1), ("z", -1)])
    sum_a = RingSum(links, "z", qa, relay_a, mid_a, near_a)
    sum_b = RingSum(links, "y", qb, relay_b, mid_b, near_b)
    sum_a.start()
    sum_b.start()
    sum_a.forward()
    sum_b.forward()

    def into(ref):
        def put(half, span, value):
            i = span.start // 16
            ref[2 * half + i // 2, lax.rem(i, 2)] = value.astype(BF16)

        return put

    sum_a.finish(into(next_a))
    sum_c = RingSum(links, "y", next_a, relay_c, mid_c, near_c)
    sum_c.start()
    sum_b.finish(into(next_b))
    sum_d = RingSum(links, "z", next_b, relay_d, mid_d, near_d)
    sum_d.start()
    sum_c.forward()
    sum_d.forward()

    def result(ref):
        def put(half, span, value):
            ref[half] = value

        return put

    sum_c.finish(result(outa))
    sum_d.finish(result(outb))
    links.finish()


def to_owners(qa, qb):
    wa, wb = qa.shape[-1], qb.shape[-1]
    dma = pltpu.SemaphoreType.DMA

    def big(w):
        return [
            pltpu.VMEM((2, 64, w), BF16),
            pltpu.VMEM((2, 64, w), BF16),
            pltpu.VMEM((2, 2, 64, w), BF16),
            pltpu.VMEM((4, 2, 16, w), BF16),
        ]

    def small(w):
        return [
            pltpu.VMEM((2, 16, w), BF16),
            pltpu.VMEM((2, 16, w), BF16),
            pltpu.VMEM((2, 2, 16, w), BF16),
        ]

    return pl.pallas_call(
        owner_kernel,
        out_shape=(
            jax.ShapeDtypeStruct((2, 16, wa), F32),
            jax.ShapeDtypeStruct((2, 16, wb), F32),
        ),
        in_specs=[VMEM, VMEM],
        out_specs=(VMEM, VMEM),
        scratch_shapes=big(wa) + big(wb) + small(wa) + small(wb) + [dma((24,)), dma((24,))],
        compiler_params=pltpu.CompilerParams(collective_id=2, has_side_effects=True),
        name="to_owners",
    )(qa, qb)


def sum_kernel(
    part, mpart, out, mout,
    half_in, ay, ry, bxz, rxz, gy, gc, mr,
    send_sems, recv_sems,
):
    links = Links(send_sems, recv_sems)
    x, y, z, c = links.x, links.y, links.z, links.c
    m16 = x * 4 + z

    def plane(k):
        d = lax.rem(m16 + k, 16)
        return {"dp": d // 4, "enc": lax.rem(d, 4)}

    barrier = pltpu.get_barrier_semaphore()
    peers = [links.peer("y", 1), links.peer("y", 2), links.peer("y", 3), links.peer("c", 0)]
    peers += [plane(k) for k in range(1, 16)]
    for peer in peers:
        pl.semaphore_signal(barrier, inc=1, device_id=peer, device_id_type=MESH)
    pl.semaphore_wait(barrier, len(peers))

    msum = [links.send("x", k, mpart, mr.at[k - 1]) for k in (1, 2, 3)]
    other = pl.ds(pl.multiple_of((1 - c) * 8, 8), 8)
    mine = pl.ds(pl.multiple_of(c * 8, 8), 8)
    swap = links.send("c", 0, part.at[other], half_in)
    swap.wait_recv()
    for b in range(4):
        cols = slice(b * 4096, (b + 1) * 4096)
        ay[b] = part[mine, cols] + half_in[:, cols]
    along = [links.send("y", k, ay.at[wrap(y + k, 4)], ry.at[k - 1]) for k in (1, 2, 3)]
    for copy in along:
        copy.wait_recv()
    mine_y = ay.at[y]
    for b in range(16):
        cols = slice(b * 256, (b + 1) * 256)
        bxz[b] = (mine_y[:, cols] + ry[0, :, cols]) + (ry[1, :, cols] + ry[2, :, cols])
    base = len(links.made)

    def spread(k):
        return pltpu.make_async_remote_copy(
            src_ref=bxz.at[lax.rem(m16 + k, 16)], dst_ref=rxz.at[k], send_sem=send_sems.at[base + k],
            recv_sem=recv_sems.at[base + k], device_id=plane(k), device_id_type=MESH,
        )

    def share(k, slot):
        return pltpu.make_async_remote_copy(
            src_ref=gy.at[y, m16], dst_ref=gy.at[y, slot], send_sem=send_sems.at[base + 16 + k],
            recv_sem=recv_sems.at[base + 16 + k], device_id=plane(k), device_id_type=MESH,
        )

    def over(act):
        def step(k, carry):
            act(k)
            return carry

        lax.fori_loop(1, 16, step, 0)

    over(lambda k: spread(k).start())
    over(lambda k: spread(k).wait_recv())
    rxz[0] = bxz[m16]
    value = rxz[0]
    for k in range(1, 16):
        value = value + rxz[k]
    gy[y, m16] = value
    over(lambda k: share(k, m16).start())
    for copy in msum:
        copy.wait_recv()
    mout[...] = (mpart[...] + mr[0]) + (mr[1] + mr[2])
    over(lambda k: share(k, lax.rem(m16 - k + 16, 16)).wait_recv())
    links.made += [None] * 32
    wide = [links.send("y", k, gy.at[y], gy.at[y]) for k in (1, 2, 3)]
    for copy in wide:
        copy.wait_recv()
    last = links.send("c", 0, gy, gc)
    for b in range(64):
        out[mine, b * 256 : (b + 1) * 256] = gy[b // 16, b % 16]
    last.wait_recv()
    for b in range(64):
        out[other, b * 256 : (b + 1) * 256] = gc[b // 16, b % 16]
    over(lambda k: spread(k).wait_send())
    over(lambda k: share(k, m16).wait_send())
    links.made = [copy for copy in links.made if copy is not None]
    links.finish()


def summed(part, mpart):
    dma = pltpu.SemaphoreType.DMA
    return pl.pallas_call(
        sum_kernel,
        out_shape=(
            jax.ShapeDtypeStruct(part.shape, F32),
            jax.ShapeDtypeStruct(mpart.shape, F32),
        ),
        in_specs=[VMEM, VMEM],
        out_specs=(VMEM, VMEM),
        scratch_shapes=[
            pltpu.VMEM((8, 16384), F32),
            pltpu.VMEM((4, 8, 4096), F32),
            pltpu.VMEM((3, 8, 4096), F32),
            pltpu.VMEM((16, 8, 256), F32),
            pltpu.VMEM((16, 8, 256), F32),
            pltpu.VMEM((4, 16, 8, 256), F32),
            pltpu.VMEM((4, 16, 8, 256), F32),
            pltpu.VMEM((3, 16, 256), F32),
            dma((48,)), dma((48,)),
        ],
        compiler_params=pltpu.CompilerParams(collective_id=3, has_side_effects=True),
        name="summed",
    )(part, mpart)


def gelu_parts(preact):
    normal_cdf = 0.5 * (1.0 + lax.erf(preact * 0.7071067811865476))
    normal_pdf = jnp.exp(-0.5 * preact * preact) * 0.3989422804014327
    return (normal_cdf, normal_pdf)


def owner_layout(image_token_counts, image_encoder_owner, owner_count, owner_room, slot_len):
    image_ids = jnp.arange(image_token_counts.shape[0])
    same_owner = image_encoder_owner[:, None] == image_encoder_owner[None, :]
    earlier = image_ids[None, :] < image_ids[:, None]
    starts = jnp.sum(jnp.where(same_owner & earlier, image_token_counts[None, :], 0), axis=1)
    row_index = jnp.arange(owner_count * owner_room)
    row_owner = row_index // owner_room
    row_place = row_index % owner_room
    matches = (
        (row_owner[:, None] == image_encoder_owner[None, :])
        & (row_place[:, None] >= starts[None, :])
        & (row_place[:, None] < (starts + image_token_counts)[None, :])
    )
    source = jnp.sum(
        jnp.where(matches, image_ids[None, :] * slot_len + row_place[:, None] - starts[None, :], 0),
        axis=1,
    )
    return jnp.where(jnp.any(matches, axis=1), source, -1)


def window(value, first):
    start = jnp.minimum(first, value.shape[0] - MAXIMG)
    rows = lax.dynamic_slice_in_dim(value, start, MAXIMG, 0)
    return lax.dynamic_slice_in_dim(jnp.concatenate([rows, rows], axis=0), first - start, MAXIMG, 0)


def body(
    hidden,
    residual_gradient,
    value_output_gradient,
    attention_norm_gain,
    value_frozen_weight,
    value_down_factor,
    value_up_factor,
    merger_frozen_weight,
    merger_down_factor,
    merger_up_factor,
    merger_saved_preactivation,
    image_token_counts,
    image_encoder_owner,
    image_first_rows,
):
    scale_factor = 256.0 / (hidden.shape[0] * 128) * adapter_scale
    x, y, z, c = place()
    member = (2 * y + c) * 4 + z
    gain = attention_norm_gain.reshape(8, 1, 1024)
    down_t = value_down_factor.T.reshape(16, 8, 1024).transpose(1, 0, 2)

    preact = merger_saved_preactivation.astype(F32)
    normal_cdf, normal_pdf = gelu_parts(preact)
    activation = (preact * normal_cdf).astype(BF16)
    act_low = jnp.dot(activation, merger_down_factor, preferred_element_type=F32).astype(BF16)
    act_low = jnp.pad(act_low, ((0, 0), (0, 112)))

    first = image_first_rows[0]
    count = lax.dynamic_index_in_dim(image_token_counts, member, 0, keepdims=False)
    keep = jnp.broadcast_to((jnp.arange(MAXIMG) < count)[:, None], (MAXIMG, 128)).astype(F32)
    vrecv, alow, wm_other, mup_other = image_chain(
        window(value_output_gradient, first),
        window(hidden, first),
        window(residual_gradient, first),
        keep,
        gain,
        value_frozen_weight,
        value_up_factor,
        down_t,
        act_low,
        merger_frozen_weight,
        merger_up_factor,
    )

    source = owner_layout(image_token_counts, image_encoder_owner, 32, 32, MAXIMG)
    mine = lax.dynamic_index_in_dim(source.reshape(4, 2, 4, 32), c, 1, keepdims=False)
    slots = jnp.arange(512)
    pick = (mine.reshape(512)[:, None] == slots[None, :]).astype(BF16)
    vis_own = lax.dynamic_index_in_dim(vrecv, c, 1, keepdims=False).reshape(512, 256)
    vis_other = lax.dynamic_index_in_dim(vrecv, 1 - c, 1, keepdims=False).reshape(512, 256)
    rows_own = jnp.dot(pick, vis_own, preferred_element_type=F32).astype(BF16)
    rows_other = jnp.dot(pick, vis_other, preferred_element_type=F32).astype(BF16)
    low_part = dot_nt(rows_own, merger_up_factor) + dot_nt(rows_other, mup_other)
    partial = (
        dot_nt(rows_own, merger_frozen_weight)
        + dot_nt(rows_other, wm_other)
        + adapter_scale * jnp.dot(low_part, merger_down_factor.astype(F32).T)
    ).astype(BF16)
    cut = 2560
    qa = partial[:, :cut].reshape(4, 4, 32, cut).transpose(1, 0, 2, 3).reshape(4, 2, 64, cut)
    qb = jnp.concatenate(
        [partial[:, cut:], jnp.pad(low_part, ((0, 0), (0, 112))).astype(BF16)], axis=1
    ).reshape(4, 2, 64, cut + 128)

    pick_all = (source[:, None] == slots[None, :]).astype(BF16)
    low_slots = dot_tn(pick_all, alow[:, :, :16].reshape(1024, 16)).astype(BF16)
    term_b2 = scale_factor * dot_tn(low_slots, vis_own)

    layer_input_gradient, down_term, up_term = main_block(
        scale_factor,
        hidden,
        residual_gradient,
        value_frozen_weight,
        value_output_gradient,
        value_up_factor,
        gain,
        down_t,
    )
    outa, outb = to_owners(qa, qb)
    combined = jnp.concatenate(
        [outa.reshape(32, cut), outb.reshape(32, cut + 128)[:, :cut]], axis=1
    )
    low_sum = outb.reshape(32, cut + 128)[:, cut : cut + 16]
    preactivation_gradient = (combined * (normal_cdf + preact * normal_pdf)).astype(BF16)
    term_a2 = scale_factor * dot_tn(low_sum.astype(BF16), activation)
    part = jnp.concatenate(
        [
            down_term.transpose(1, 0, 2).reshape(16, 8192),
            up_term,
            term_a2,
            jnp.zeros((16, 2048), F32),
        ],
        axis=1,
    )
    sums, merger_up_gradient = summed(part, term_b2)
    return (
        layer_input_gradient,
        preactivation_gradient,
        sums[:, :8192].T,
        sums[:, 8192:9216],
        sums[:, 9216:14336].T,
        merger_up_gradient,
    )


def solution(mesh):
    tokens = P(("dp", "fsdp", "enc"), None)
    features = P(None, ("fsdp", "enc"))
    placed = (
        tokens,
        tokens,
        tokens,
        P(),
        P("fsdp", None),
        P(),
        P(),
        features,
        P(),
        features,
        tokens,
        P("dp"),
        P("dp"),
        P(("dp", "fsdp", "enc")),
    )
    return jax.shard_map(
        body,
        mesh=mesh,
        in_specs=placed,
        out_specs=(tokens, tokens, P(), P(), P(), features),
        check_vma=False,
    )
```

time: 478 us -> 220 us (0.46)
  waiting for transfers between devices: 337 us -> 0 us
  Pallas kernels: 0 us -> 164 us
  matrix products: 49.1 us -> 19.6 us
  blocking collectives: 21.8 us -> 0 us
  other arithmetic: 27.4 us -> 10.4 us
  between operations: 14.7 us -> 1.63 us
  starting transfers between devices: 11.3 us -> 0 us
  local copies, waits for them, and re-layouts: 15.8 us -> 23 us
    pallas_call x0 -> x4, Pallas kernels: none -> 164 us  [the longest x1 58.8 us: main_block(): pl.pallas_call(functools.partial(main_kernel, scale_factor), out_shape=(j...]
    psum x1 -> x0, waiting for transfers between devices: 127 us -> none  [body(): lax.psum((scale_factor * down_term, scale_factor * up_term, scale_factor...]
    reduce_scatter x1 -> x0, waiting for transfers between devices: 118 us -> none  [in_one_piece(): out = lax.psum_scatter(both, axis, scatter_dimension=dim, tiled=True)]
    all_to_all x2 -> x0, waiting for transfers between devices: 54.7 us -> none  [the longest x1 46.3 us: body(): lax.all_to_all(columns, 'fsdp', split_axis=0, concat_axis=1, tiled=True)]
    all_gather x1 -> x0, waiting for transfers between devices: 37.5 us -> none  [body(): lax.all_gather(value_output_gradient, 'fsdp', axis=0, tiled=True)]
    dot_general x11 -> x10, matrix products: 49.1 us -> 19.6 us  [the longest x4 9.37 us: dot_nt(): lax.dot_general(a, b, (((1,), (1,)), ((), ())), preferred_element_type=F32)]
    all_to_all x2 -> x0, blocking collectives: 21.8 us -> none  [sent_to_all(): return lax.all_to_all(copies, axis, split_axis=0, concat_axis=0, tiled=True)]
    all_to_all x2 -> x0, starting transfers between devices: 11 us -> none  [the longest x1 6.13 us: body(): lax.all_to_all(slots_out, ('fsdp', 'enc'), split_axis=1, concat_axis=0, t...]
  transfers between devices with their start and end apart: 5 -> 0, of which waited for: 5 -> 0; matrix products, arithmetic and copies ran while one was open for 3% -> 0% of each run, Pallas kernels for 0% -> 0%
where the time goes in v1:
time: 220 us; the launch traced here: 219 us
  Pallas kernels  164 us (75%)
  local copies, waits for them, and re-layouts  23 us (10%)
  matrix products  19.6 us (9%)
  other arithmetic  10.4 us (5%)
    pallas_call x1, Pallas kernels, main_block(): pl.pallas_call(functools.partial(main_kernel, scale_factor), out_shape=(j...  58.8 us
    pallas_call x1, Pallas kernels, to_owners(): pl.pallas_call(owner_kernel, out_shape=(jax.ShapeDtypeStruct((2, 16, wa),...  38.5 us
    pallas_call x1, Pallas kernels, summed(): pl.pallas_call(sum_kernel, out_shape=(jax.ShapeDtypeStruct(part.shape, F3...  33.9 us
    pallas_call x1, Pallas kernels, image_chain(): pl.pallas_call(image_kernel, out_shape=(jax.ShapeDtypeStruct((32, 2, 16,...  33.2 us
    dot_general x4, matrix products, dot_nt(): lax.dot_general(a, b, (((1,), (1,)), ((), ())), preferred_element_type=F32)  9.37 us
    dot_general x1, matrix products, body(): jnp.dot(low_part, merger_down_factor.astype(F32).T)  6.03 us
    unnamed x33, local copies, waits for them, and re-layouts  5.5 us

profile of v1, /device:TPU:1, one launch (start us, length us, event | category | flops | bytes accessed | tf_op | source)
XLA Modules:
  0.0 219.0 jit_solution(15683538113940280664)
XLA Ops:
  0.6 0.0 copy-start
  0.7 1.3 dynamic_slice.40
  2.0 0.6 compare_convert_fusion
  2.6 0.7 broadcast_in_dim.23.keep
  4.0 1.1 constant_dynamic-slice_fusion.1
  5.0 1.1 constant_dynamic-slice_fusion.2
  6.1 1.2 fusion.17
  7.3 0.8 constant_dynamic-slice_fusion.4
  8.1 0.7 fusion.19.vimg
  8.8 1.1 fusion.8
  9.9 0.0 copy-start.12
  9.9 0.0 copy-start.13
  9.9 1.2 convolution_convert_fusion.2
  11.1 0.1 copy.38
  11.1 0.6 pad.9.act_low
  11.8 0.7 copy.46
  12.5 33.2 %image_chain.1 = (bf16[32,2,16,256]{3,2,1,0:T(8,128)(2,1)}, bf16[32,32,128]{2,1,0:T(8,128)(2,1)}, bf16[5120,256]{1,0:T(8,128)(2,1)}, bf16[16,256]{1,0:T(8,128)(2,1)}) custom-call(bf16[16,1024]{1,0:T(8,128)(2,1)} %fusion.19.vimg, bf16[16,8192]{1,0:T(8,128)(2,1)} %get-tuple-element.35.ximg, bf16[16,8192]{1,0:T(8,128)(2,1)} %get-tuple-element.34.rimg, ...), custom_call_target="tpu_custom_call" | custom-call | tf_op jit(solution)/shard_map/image_chain/pallas_call | solution.py:189
  45.7 1.1 constant_dynamic-slice_fusion.3
  46.9 0.2 select_reduce_fusion.1
  47.1 0.1 select_reduce_fusion
  47.2 0.1 fusion.28
  47.3 0.1 select_n.76
  47.4 0.1 eq.62
  47.5 0.4 convolution_convert_fusion
  47.9 0.0 copy-start.2
  47.9 3.5 %fusion.33 = f32[512,5120]{1,0:T(8,128)S(1)} fusion(bf16[512,256]{1,0:T(8,128)(2,1)S(1)} %convolution_convert_fusion, bf16[5120,256]{1,0:T(8,128)(2,1)} %get-tuple-element.19), kind=kOutput, calls=%fused_computation.73 | convolution fusion | flops 1342177280 | bytes 13369344 | tf_op jit(solution)/shard_map/dot_general | solution.py:20
  51.4 0.4 convolution_convert_fusion.1
  51.8 0.2 fusion.34
  51.9 0.2 convolution_add_fusion
  52.1 5.6 %fusion.32 = f32[512,5120]{1,0:T(8,128)} fusion(bf16[512,256]{1,0:T(8,128)(2,1)S(1)} %convolution_convert_fusion.1, bf16[5120,256]{1,0:T(8,128)(2,1)S(1)} %copy-done.2), kind=kOutput, calls=%fused_computation.72 | convolution fusion | flops 1342177280 | bytes 13369344 | tf_op jit(solution)/shard_map/dot_general | solution.py:20
  57.7 6.0 %add_convert_fusion = bf16[512,5120]{1,0:T(8,128)(2,1)S(1)} fusion(f32[512,5120]{1,0:T(8,128)} %fusion.32, f32[512,5120]{1,0:T(8,128)S(1)} %fusion.33, bf16[512,16]{0,1:T(8,128)(2,1)S(1)} %convolution_add_fusion, bf16[5120,16]{0,1:T(8,128)(2,1)S(1)} %copy-done), kind=kOutput, calls=%fused_computation | convolution fusion | flops 94371840 | bytes 26394624 | tf_op jit(solution)/shard_map/dot_general | solution.py:743
  63.7 1.9 fusion.31
  65.6 0.1 copy.42
  65.7 3.5 %fusion.1 = bf16[512,2688]{1,0:T(8,128)(2,1)} fusion(bf16[512,16]{1,0:T(8,128)(2,1)S(1)} %copy.42, bf16[512,2560]{1,0:T(8,128)(2,1)} %get-tuple-element.28), kind=kLoop, calls=%fused_computation.4 | loop fusion | flops 8257536 | bytes 5390336 | tf_op jit(solution)/shard_map/concatenate | solution.py:747
  69.2 1.7 copy.39
  70.9 38.5 %to_owners.1 = (f32[2,16,2560]{2,1,0:T(8,128)}, f32[2,16,2688]{2,1,0:T(8,128)}) custom-call(bf16[4,2,64,2560]{3,2,1,0:T(8,128)(2,1)} %bitcast.48, bf16[4,2,64,2688]{3,2,1,0:T(8,128)(2,1)} %bitcast.46), custom_call_target="tpu_custom_call" | custom-call | tf_op jit(solution)/shard_map/to_owners/pallas_call | solution.py:530
  109.4 0.9 convolution_multiply_fusion
  110.4 58.8 %main_block.1 = (bf16[256,8192]{1,0:T(8,128)(2,1)}, f32[8,16,1024]{2,1,0:T(8,128)}, f32[16,1024]{1,0:T(8,128)}) custom-call(bf16[256,8192]{1,0:T(8,128)(2,1)} %hidden.1, bf16[256,8192]{1,0:T(8,128)(2,1)} %resid.1, bf16[1024,1024]{1,0:T(8,128)(2,1)} %wsh.3, bf16[256,1024]{1,0:T(8,128)(2,1)} %v.1, bf16[16,1024]{1,0:T(8,128)(2,1)} %up.3, ...), custom_call_target="tpu_custom_call" | custom-call | tf_op jit(solution)/shard_map/main_block/pallas_call | solution.py:386
  169.2 1.1 copy.44
  170.4 1.9 maximum_maximum_fusion.part
  172.3 1.4 convolution_multiply_fusion.1.mpart
  173.6 33.9 %summed.1 = (f32[16,16384]{1,0:T(8,128)}, f32[16,256]{1,0:T(8,128)}) custom-call(f32[16,16384]{1,0:T(8,128)} %maximum_maximum_fusion.part, f32[16,256]{1,0:T(8,128)} %convolution_multiply_fusion.1.mpart), custom_call_target="tpu_custom_call" | custom-call | tf_op jit(solution)/shard_map/summed/pallas_call | solution.py:630
  207.5 1.9 slice_bitcast_fusion
  209.4 1.7 slice_bitcast_fusion.1
  211.1 1.5 slice.31
  212.6 1.0 fusion.14
  213.7 4.7 %copy.50 = bf16[256,8192]{1,0:T(8,128)(2,1)} copy(bf16[256,8192]{1,0:T(8,128)(2,1)} %get-tuple-element.42) | data formatting | bytes 8388608
  218.3 0.6 copy.51
  (34 shorter events, 0.1 us)
Async XLA Ops:
  0.6 9.2 %copy-start = (bf16[5120,16]{0,1:T(8,128)(2,1)S(1)}, bf16[5120,16]{0,1:T(8,128)(2,1)}, u32[]{:S(2)}) copy-start(bf16[5120,16]{0,1:T(8,128)(2,1)} %param.22) | copy-start | bytes 491524
  0.6 11.1 %copy-start.8 = (bf16[8192,16]{0,1:T(8,128)(2,1)S(1)}, bf16[8192,16]{0,1:T(8,128)(2,1)}, u32[]{:S(2)}) copy-start(bf16[8192,16]{0,1:T(8,128)(2,1)} %param.19) | copy-start | bytes 786436
  9.9 37.0 %copy-start.12 = (s32[32]{0:T(128)S(1)}, s32[32]{0:T(128)}, u32[]{:S(2)}) copy-start(s32[32]{0:T(128)} %param.26) | copy-start | bytes 388
  9.9 37.0 %copy-start.13 = (s32[32]{0:T(128)S(1)}, s32[32]{0:T(128)}, u32[]{:S(2)}) copy-start(s32[32]{0:T(128)} %param.25) | copy-start | bytes 388
  46.8 4.5 %copy-start.6 = (bf16[32,1,16,256]{3,2,1,0:T(8,128)(2,1)}, bf16[32,1,16,256]{3,2,1,0:T(8,128)(2,1)S(1)}, u32[]{:S(2)}) copy-start(bf16[32,1,16,256]{3,2,1,0:T(8,128)(2,1)S(1)} %get-tuple-element.31) | copy-start | bytes 786436
  47.9 3.9 %copy-start.9 = (bf16[16,256]{1,0:T(8,128)(2,1)S(1)}, bf16[16,256]{1,0:T(8,128)(2,1)}, u32[]{:S(2)}) copy-start(bf16[16,256]{1,0:T(8,128)(2,1)} %mup.1) | copy-start | bytes 24580
  47.9 4.0 %copy-start.11 = (bf16[16,256]{1,0:T(8,128)(2,1)S(1)}, bf16[16,256]{1,0:T(8,128)(2,1)}, u32[]{:S(2)}) copy-start(bf16[16,256]{1,0:T(8,128)(2,1)} %get-tuple-element.20) | copy-start | bytes 24580
  47.9 4.2 %copy-start.2 = (bf16[5120,256]{1,0:T(8,128)(2,1)S(1)}, bf16[5120,256]{1,0:T(8,128)(2,1)}, u32[]{:S(2)}) copy-start(bf16[5120,256]{1,0:T(8,128)(2,1)} %wm.1) | copy-start | bytes 7864324
  70.9 38.5 %copy-start.3 = (bf16[32,5120]{1,0:T(8,128)(2,1)S(1)}, bf16[32,5120]{1,0:T(8,128)(2,1)}, u32[]{:S(2)}) copy-start(bf16[32,5120]{1,0:T(8,128)(2,1)} %param.24) | copy-start | bytes 983044
  110.4 61.9 %copy-start.7 = (bf16[32,1,16,256]{3,2,1,0:T(8,128)(2,1)S(1)}, bf16[32,1,16,256]{3,2,1,0:T(8,128)(2,1)}, u32[]{:S(2)}) copy-start(bf16[32,1,16,256]{3,2,1,0:T(8,128)(2,1)} %copy-done.6) | copy-start | bytes 786436
  110.4 61.9 %copy-start.14 = (bf16[32,32,128]{2,1,0:T(8,128)(2,1)S(1)}, bf16[32,32,128]{2,1,0:T(8,128)(2,1)}, u32[]{:S(2)}) copy-start(bf16[32,32,128]{2,1,0:T(8,128)(2,1)} %get-tuple-element.25) | copy-start | bytes 786436
  169.2 43.4 %copy-start.4 = (f32[2,16,2688]{2,1,0:T(8,128)S(1)}, f32[2,16,2688]{2,1,0:T(8,128)}, u32[]{:S(2)}) copy-start(f32[2,16,2688]{2,1,0:T(8,128)} %get-tuple-element.22) | copy-start | bytes 1032196
  169.2 43.5 %copy-start.5 = (f32[2,16,2560]{2,1,0:T(8,128)S(1)}, f32[2,16,2560]{2,1,0:T(8,128)}, u32[]{:S(2)}) copy-start(f32[2,16,2560]{2,1,0:T(8,128)} %get-tuple-element.21) | copy-start | bytes 983044
  213.6 5.3 %copy-start.1 = (bf16[5120,16]{0,1:T(8,128)(2,1)S(1)}, bf16[5120,16]{0,1:T(8,128)(2,1)}, u32[]{:S(2)}) copy-start(bf16[5120,16]{0,1:T(8,128)(2,1)} %param.22) | copy-start | bytes 491524
  213.7 4.7 %copy-start.10 = (f32[16,256]{1,0:T(8,128)S(1)}, f32[16,256]{1,0:T(8,128)}, u32[]{:S(2)}) copy-start(f32[16,256]{1,0:T(8,128)} %get-tuple-element.47) | copy-start | bytes 49156

commit v2 on v0

v2 whole, which is shorter than its diff:
```python
import functools

import jax
import jax.numpy as jnp
from jax import lax
from jax.experimental import pallas as pl
from jax.experimental.pallas import tpu as pltpu
from jax.sharding import PartitionSpec as P

MAXIMG = 16
adapter_scale = 2.0
norm_eps = 1e-06
F32, BF16 = jnp.float32, jnp.bfloat16
MESH = pl.DeviceIdType.MESH
VMEM = pl.BlockSpec(memory_space=pltpu.VMEM)
ANY = pl.BlockSpec(memory_space=pl.ANY)


def dot_nt(a, b):
    return lax.dot_general(a, b, (((1,), (1,)), ((), ())), preferred_element_type=F32)


def dot_tn(a, b):
    return lax.dot_general(a, b, (((0,), (0,)), ((), ())), preferred_element_type=F32)


def wrap(v, n):
    return lax.rem(v + n, n)


def place():
    f = lax.axis_index("fsdp")
    return lax.axis_index("dp"), f // 2, lax.axis_index("enc"), lax.rem(f, 2)


class Links:
    def __init__(self, send_sems, recv_sems):
        self.x, self.y, self.z, self.c = place()
        self.send_sems, self.recv_sems = send_sems, recv_sems
        self.made = []

    def peer(self, axis, step):
        if axis == "x":
            return {"dp": wrap(self.x + step, 4)}
        if axis == "z":
            return {"enc": wrap(self.z + step, 4)}
        if axis == "y":
            return {"fsdp": 2 * wrap(self.y + step, 4) + self.c}
        return {"fsdp": 2 * self.y + 1 - self.c}

    def send(self, axis, step, src, dst):
        k = len(self.made)
        copy = pltpu.make_async_remote_copy(
            src_ref=src,
            dst_ref=dst,
            send_sem=self.send_sems.at[k],
            recv_sem=self.recv_sems.at[k],
            device_id=self.peer(axis, step),
            device_id_type=MESH,
        )
        copy.start()
        self.made.append(copy)
        return copy

    def finish(self):
        for copy in self.made:
            copy.wait_send()

    def meet(self, peers):
        barrier = pltpu.get_barrier_semaphore()
        for axis, step in peers:
            pl.semaphore_signal(barrier, inc=1, device_id=self.peer(axis, step), device_id_type=MESH)
        pl.semaphore_wait(barrier, len(peers))


def chunked(count, act):
    def step(i, carry):
        act(pl.ds(pl.multiple_of(i * 16, 16), 16))
        return carry

    lax.fori_loop(0, count // 16, step, 0)


class RingSum:
    def __init__(self, links, axis, blocks, relay, mid, near):
        self.links, self.axis, self.blocks = links, axis, blocks
        self.relay, self.mid, self.near = relay, mid, near
        m = links.x if axis == "x" else links.y if axis == "y" else links.z
        self.me, self.count = m, blocks.shape[2]

    def start(self):
        send, b, axis = self.links.send, self.blocks, self.axis
        far = wrap(self.me + 2, 4)
        right, left = wrap(self.me + 1, 4), wrap(self.me - 1, 4)
        self.far = [
            send(axis, 1, b.at[far, 0], self.relay.at[0]),
            send(axis, -1, b.at[far, 1], self.relay.at[1]),
        ]
        self.direct = [
            send(axis, 1, b.at[right, 1], self.near.at[0, 1]),
            send(axis, -1, b.at[left, 0], self.near.at[1, 0]),
        ]

    def forward(self):
        for way, step in ((0, 1), (1, -1)):
            self.far[way].wait_recv()
            to = wrap(self.me + step, 4)

            def add(span, way=way, to=to):
                self.mid[way, span] = (
                    self.blocks[to, way, span].astype(F32) + self.relay[way, span].astype(F32)
                ).astype(BF16)

            chunked(self.count, add)
            self.direct.append(
                self.links.send(self.axis, step, self.mid.at[way], self.near.at[way, way])
            )

    def finish(self, put):
        for copy in self.direct:
            copy.wait_recv()
        for half in range(2):

            def add(span, half=half):
                put(
                    half,
                    span,
                    self.blocks[self.me, half, span].astype(F32)
                    + self.near[0, half, span].astype(F32)
                    + self.near[1, half, span].astype(F32),
                )

            chunked(self.count, add)


class AdapterSum:
    def __init__(self, links, src, out, bufs, sems):
        self.links, self.src, self.out = links, src, out
        self.half_in, self.ay, self.ry, self.bxz, self.rxz, self.gy, self.gc = bufs
        self.sems = sems
        self.m16 = links.x * 4 + links.z
        self.other = pl.ds(pl.multiple_of((1 - links.c) * 8, 8), 8)
        self.mine = pl.ds(pl.multiple_of(links.c * 8, 8), 8)

    def plane(self, k):
        d = lax.rem(self.m16 + k, 16)
        return {"dp": d // 4, "enc": lax.rem(d, 4)}

    def spread(self, k):
        return pltpu.make_async_remote_copy(
            src_ref=self.bxz.at[lax.rem(self.m16 + k, 16)], dst_ref=self.rxz.at[k],
            send_sem=self.sems[0].at[k], recv_sem=self.sems[1].at[k],
            device_id=self.plane(k), device_id_type=MESH,
        )

    def share(self, k, slot):
        return pltpu.make_async_remote_copy(
            src_ref=self.gy.at[self.links.y, self.m16], dst_ref=self.gy.at[self.links.y, slot],
            send_sem=self.sems[2].at[k], recv_sem=self.sems[3].at[k],
            device_id=self.plane(k), device_id_type=MESH,
        )

    def swap(self):
        self.swapped = self.links.send("c", 0, self.src.at[self.other], self.half_in)

    def along(self):
        self.swapped.wait_recv()
        for b in range(4):
            cols = slice(b * 2048, (b + 1) * 2048)
            self.ay[b] = self.src[self.mine, cols] + self.half_in[:, cols]
        y = self.links.y
        self.sent = [
            self.links.send("y", k, self.ay.at[wrap(y + k, 4)], self.ry.at[k - 1]) for k in (1, 2, 3)
        ]

    def across(self):
        for copy in self.sent:
            copy.wait_recv()
        here = self.ay.at[self.links.y]
        for b in range(16):
            cols = slice(b * 128, (b + 1) * 128)
            self.bxz[b] = (here[:, cols] + self.ry[0, :, cols]) + (
                self.ry[1, :, cols] + self.ry[2, :, cols]
            )
        over(1, 16, lambda k: self.spread(k).start())

    def back(self):
        over(1, 16, lambda k: self.spread(k).wait_recv())
        value = self.bxz[self.m16]
        for k in range(1, 16):
            value = value + self.rxz[k]
        self.gy[self.links.y, self.m16] = value
        over(1, 16, lambda k: self.share(k, self.m16).start())

    def outward(self):
        over(1, 16, lambda k: self.share(k, lax.rem(self.m16 - k + 16, 16)).wait_recv())
        y = self.links.y
        self.wide = [self.links.send("y", k, self.gy.at[y], self.gy.at[y]) for k in (1, 2, 3)]

    def last(self):
        for copy in self.wide:
            copy.wait_recv()
        self.final = self.links.send("c", 0, self.gy, self.gc)
        for b in range(64):
            self.out[self.mine, b * 128 : (b + 1) * 128] = self.gy[b // 16, b % 16]

    def end(self):
        self.final.wait_recv()
        for b in range(64):
            self.out[self.other, b * 128 : (b + 1) * 128] = self.gc[b // 16, b % 16]
        over(1, 16, lambda k: self.spread(k).wait_send())
        over(1, 16, lambda k: self.share(k, self.m16).wait_send())


def over(lo, hi, act):
    def step(j, carry):
        act(j)
        return carry

    lax.fori_loop(lo, hi, step, 0)


def big_kernel(
    scale_factor,
    first_row, counts_s, counts, owners, v, up, gain, down_t, preact, md, mup,
    hidden, resid, wsh, wm,
    through_out, low_out_ref, inverse_out, drop_out, outa, outb, sums1, sums2, mout,
    wbuf, xb, rb, through, send_sems, recv_sems, local_sems, out_sems,
    vimg, xsel, rsel, vall, tout, timg, gained, visout, vrecv, actl, alow, act,
    s1, r1, s2, r2, s3, r3, s4, r4,
    wmb, mup_other, lowp, lowin, s5, r5, rows_own, rows_other, mpart, mr,
    qa, qb,
    relay_a, mid_a, near_a, next_a, relay_b, mid_b, near_b, next_b,
    relay_c, mid_c, near_c, relay_d, mid_d, near_d,
    part1, part2, *rest,
):
    bufs1, bufs2, sems1, sems2 = rest[:7], rest[7:14], rest[14:18], rest[18:22]
    links = Links(send_sems, recv_sems)
    x, y, z, c = links.x, links.y, links.z, links.c
    f = 2 * y + c
    me = f * 4 + z

    own = pltpu.make_async_copy(wsh, wbuf.at[c, 0], local_sems.at[0])
    own.start()
    loads = []
    for k in range(8):
        cols = pl.ds(k * 1024, 1024)
        a = pltpu.make_async_copy(hidden.at[:, cols], xb.at[k], local_sems.at[1 + k])
        b = pltpu.make_async_copy(resid.at[:, cols], rb.at[k], local_sems.at[9 + k])
        a.start()
        b.start()
        loads.append((a, b))
    wm_load = pltpu.make_async_copy(wm, wmb.at[0], local_sems.at[17])
    wm_load.start()

    barrier = pltpu.get_barrier_semaphore()

    def plane_peer(j):
        d = lax.rem(me + j, 32)
        return {"fsdp": d // 4, "enc": lax.rem(d, 4)}

    def greet(j):
        pl.semaphore_signal(barrier, inc=1, device_id=plane_peer(j), device_id_type=MESH)

    def greet_x(j):
        d = 4 + j
        pl.semaphore_signal(
            barrier,
            inc=1,
            device_id={"dp": lax.rem(x + d // 4, 4), "enc": lax.rem(z + d, 4)},
            device_id_type=MESH,
        )

    over(1, 32, greet)
    over(0, 12, greet_x)
    first = first_row[0]
    lane = lax.broadcasted_iota(jnp.int32, (16, 256), 1)
    line = lax.broadcasted_iota(jnp.int32, (16, 256), 0)
    sel = jnp.where(lane == line + first, 1.0, 0.0).astype(BF16)
    vimg[...] = jnp.dot(sel, v[...], preferred_element_type=F32).astype(BF16)
    pl.semaphore_wait(barrier, 43)

    def row(j, slot):
        return pltpu.make_async_remote_copy(
            src_ref=vimg, dst_ref=vall.at[slot], send_sem=s1.at[j], recv_sem=r1.at[j],
            device_id={"fsdp": lax.rem(f + j, 8)}, device_id_type=MESH,
        )

    def back(j, slot):
        return pltpu.make_async_remote_copy(
            src_ref=tout.at[lax.rem(f + j, 8)], dst_ref=timg.at[slot], send_sem=s2.at[j],
            recv_sem=r2.at[j], device_id={"fsdp": lax.rem(f + j, 8)}, device_id_type=MESH,
        )

    def spread(j, slot):
        d = lax.rem(me + j, 32)
        return pltpu.make_async_remote_copy(
            src_ref=visout.at[d // 8, lax.rem(d, 4)], dst_ref=vrecv.at[slot], send_sem=s3.at[j],
            recv_sem=r3.at[j], device_id=plane_peer(j), device_id_type=MESH,
        )

    def low_out(j, slot):
        return pltpu.make_async_remote_copy(
            src_ref=actl, dst_ref=alow.at[slot], send_sem=s4.at[j], recv_sem=r4.at[j],
            device_id=plane_peer(j), device_id_type=MESH,
        )

    my16 = y * 4 + z

    def low_row(j, slot):
        d = lax.rem(my16 + j, 16)
        return pltpu.make_async_remote_copy(
            src_ref=lowp.at[d], dst_ref=lowin.at[slot], send_sem=s5.at[j], recv_sem=r5.at[j],
            device_id={"fsdp": 2 * (d // 4) + c, "enc": lax.rem(d, 4)}, device_id_type=MESH,
        )

    def at(j, start, count):
        return wbuf.at[c, j, pl.ds(pl.multiple_of(start, 16), count)]

    def piece(step):
        return (x * 4 + wrap(z + step, 4)) * 64

    def block(step):
        return wrap(x + step, 4) * 256

    moved = {}

    def arrived(name):
        for copy in moved[name]:
            copy.wait_recv()

    def start_y1():
        src = at(0, piece(0), 64)
        moved["y1"] = [
            links.send("y", 1, src, at(3, piece(0), 64)),
            links.send("y", -1, src, at(1, piece(0), 64)),
        ]

    def start_y2():
        moved["y2"] = [
            links.send("y", 1, at(3, piece(0), 32), at(2, piece(0), 32)),
            links.send("y", -1, at(1, piece(0) + 32, 32), at(2, piece(0) + 32, 32)),
        ]

    def start_a1(j):
        here = at(j, piece(0), 64)
        moved["a1", j] = [links.send("z", step, here, here) for step in (1, -1)]

    def start_a2(j):
        one, two = at(j, piece(-1), 32), at(j, piece(1) + 32, 32)
        moved["a2", j] = [links.send("z", 1, one, one), links.send("z", -1, two, two)]

    def start_b1(j):
        here = at(j, block(0), 256)
        moved["b1", j] = [links.send("x", step, here, here) for step in (1, -1)]

    def start_b2(j):
        one, two = at(j, block(-1), 128), at(j, block(1) + 128, 128)
        moved["b2", j] = [links.send("x", 1, one, one), links.send("x", -1, two, two)]

    def start_core(j):
        moved["core", j] = [links.send("c", 0, wbuf.at[c, j], wbuf.at[c, j])]

    over(1, 8, lambda j: row(j, f).start())
    own.wait()
    start_y1()
    wide = links.send("c", 0, wm, wmb.at[1])
    thin = links.send("c", 0, mup, mup_other)
    start_core(0)
    vall[f] = vimg[...]

    low_img = dot_nt(vimg[...], up[...]).astype(BF16)
    squares_img = jnp.zeros((16, 1), F32)
    for k in range(8):
        loads[k][0].wait()
        rows = jnp.dot(sel, xb[k], preferred_element_type=F32)
        xsel[k] = rows.astype(BF16)
        squares_img = squares_img + jnp.sum(rows * rows, axis=1, keepdims=True)
    inverse_img = lax.rsqrt(squares_img * (1.0 / 8192) + norm_eps)

    over(1, 8, lambda j: row(j, lax.rem(f - j + 8, 8)).wait_recv())
    tout[...] = dot_nt(vall[...].reshape(128, 1024), wbuf[c, 0]).astype(BF16).reshape(8, 16, 1024)
    over(1, 8, lambda j: back(j, f).start())
    timg[f] = tout[f]
    arrived("y1")
    start_y2()
    start_a1(3)
    start_a1(1)

    for k in range(8):
        loads[k][1].wait()
        rsel[k] = jnp.dot(sel, rb[k], preferred_element_type=F32).astype(BF16)
    squares = jnp.zeros((256, 1), F32)
    for k in range(8):
        xs = xb[k].astype(F32)
        squares = squares + jnp.sum(xs * xs, axis=1, keepdims=True)
    inverse = lax.rsqrt(squares * (1.0 / 8192) + norm_eps)

    over(1, 8, lambda j: back(j, lax.rem(f - j + 8, 8)).wait_recv())
    total_img = jnp.zeros((16, 1), F32)
    for k in range(8):
        grad = timg[k].astype(F32) + adapter_scale * jnp.dot(
            low_img, down_t[k], preferred_element_type=F32
        )
        g = gain[k] * grad
        gained[k] = g
        total_img = total_img + jnp.sum(xsel[k].astype(F32) * g, axis=1, keepdims=True)
    drop_img = inverse_img * inverse_img * inverse_img * (total_img * (1.0 / 8192))
    inside = lax.broadcasted_iota(jnp.int32, (16, 1024), 0) < counts_s[me]
    for k in range(8):
        rows = (
            rsel[k].astype(F32) + inverse_img * gained[k] - xsel[k].astype(F32) * drop_img
        )
        rows = jnp.where(inside, rows, 0.0).astype(BF16)
        for b in range(4):
            visout[k // 2, b, k % 2] = rows[:, b * 256 : (b + 1) * 256]
    over(1, 32, lambda j: spread(j, me).start())
    vrecv[me] = visout[y, z]

    p = preact[...].astype(F32)
    act[...] = (p * (0.5 * (1.0 + lax.erf(p * 0.7071067811865476)))).astype(BF16)
    actl[...] = jnp.zeros_like(actl)
    actl[:, 0:16] = dot_nt(act[...], md[...]).astype(BF16)
    over(1, 32, lambda j: low_out(j, me).start())
    alow[me] = actl[...]

    arrived("y2")
    start_a1(2)
    arrived(("a1", 3))
    start_a2(3)
    arrived(("a1", 1))
    start_a2(1)

    low = dot_nt(v[...], up[...]).astype(BF16)
    low_out_ref[...] = low
    low_t = dot_nt(up[...], v[...]).astype(BF16)
    projected_t = jnp.zeros((16, 256), F32)
    for k in range(8):
        normed = (xb[k].astype(F32) * inverse * gain[k]).astype(BF16)
        part1[:, k * 1024 : (k + 1) * 1024] = scale_factor * jnp.dot(
            low_t, normed, preferred_element_type=F32
        )
        projected_t = projected_t + dot_nt(down_t[k], normed)
    sum1 = AdapterSum(links, part1, sums1, bufs1, sems1)
    sum1.swap()
    arrived(("a2", 3))
    start_b1(3)
    arrived(("a1", 2))
    start_a2(2)
    arrived(("a2", 1))
    start_b1(1)
    part2[:, 0:1024] = scale_factor * jnp.dot(
        projected_t.astype(BF16), v[...], preferred_element_type=F32
    )
    part2[:, 6144:8192] = jnp.zeros((16, 2048), F32)
    sum1.along()

    eye = lax.broadcasted_iota(jnp.int32, (32, 32), 0) == lax.broadcasted_iota(
        jnp.int32, (32, 32), 1
    )
    earlier = lax.broadcasted_iota(jnp.int32, (32, 32), 1) < lax.broadcasted_iota(
        jnp.int32, (32, 32), 0
    )
    counts_f = counts[...].astype(F32)
    owners_f = owners[...].astype(F32)
    owner_col = jnp.sum(jnp.where(eye, owners_f, 0.0), axis=1, keepdims=True)
    count_col = jnp.sum(jnp.where(eye, counts_f, 0.0), axis=1, keepdims=True)
    start_col = jnp.sum(
        jnp.where((owner_col == owners_f) & earlier, counts_f, 0.0), axis=1, keepdims=True
    )
    slot = lax.broadcasted_iota(jnp.int32, (32, 512), 1)
    image = lax.broadcasted_iota(jnp.int32, (32, 512), 0)
    inner = (slot % 16).astype(F32)
    key = (
        jnp.sum(
            jnp.where(
                (slot // 16 == image) & (inner < count_col),
                owner_col * 32.0 + start_col + inner + 1.0,
                0.0,
            ),
            axis=0,
            keepdims=True,
        )
        - 1.0
    )

    over(1, 32, lambda j: spread(j, lax.rem(me - j + 32, 32)).wait_recv())
    wide.wait_recv()
    thin.wait_recv()
    wm_load.wait()
    r = lax.broadcasted_iota(jnp.int32, (512, 1), 0)
    row_id = ((2 * (r // 128) + c) * 4 + (r // 32) % 4) * 32 + r % 32
    pick = jnp.where(row_id.astype(F32) == key, 1.0, 0.0).astype(BF16)
    rows_own[...] = jnp.dot(
        pick, vrecv[:, c].reshape(512, 256), preferred_element_type=F32
    ).astype(BF16)
    rows_other[...] = jnp.dot(
        pick, vrecv[:, 1 - c].reshape(512, 256), preferred_element_type=F32
    ).astype(BF16)
    low_part = dot_nt(rows_own[...], mup[...]) + dot_nt(rows_other[...], mup_other[...])
    lowp[...] = jnp.zeros_like(lowp)
    lowp[:, :, 0:16] = low_part.reshape(16, 32, 16)
    over(1, 16, lambda j: low_row(j, my16).start())
    low_hi = low_part.astype(BF16)
    low_lo = (low_part - low_hi.astype(F32)).astype(BF16)

    def columns(n):
        cols = pl.ds(pl.multiple_of(n * 512, 512), 512)
        value = dot_nt(rows_own[...], wmb[0, cols]) + dot_nt(rows_other[...], wmb[1, cols])
        value = value + adapter_scale * (
            jnp.dot(low_hi, md[:, cols], preferred_element_type=F32)
            + jnp.dot(low_lo, md[:, cols], preferred_element_type=F32)
        )
        return value.astype(BF16)

    def fill_a(n):
        value = columns(n)
        cols = pl.ds(pl.multiple_of(n * 512, 512), 512)
        for yy in range(4):
            for zz in range(4):
                at_row = yy * 128 + zz * 32
                qa[zz, yy // 2, (yy % 2) * 32 : (yy % 2) * 32 + 32, cols] = value[
                    at_row : at_row + 32
                ]

    def fill_b(n):
        value = columns(n + 5)
        cols = pl.ds(pl.multiple_of(n * 512, 512), 512)
        qb[:, :, :, cols] = value.reshape(4, 2, 64, 512)

    sum_a = RingSum(links, "z", qa, relay_a, mid_a, near_a)
    sum_b = RingSum(links, "y", qb, relay_b, mid_b, near_b)
    over(0, 5, fill_a)
    sum_a.start()
    over(0, 5, fill_b)
    sum_b.start()

    total = jnp.zeros((256, 1), F32)
    stores = []

    def through_block(cs, j, total):
        k = 2 * lax.rem(y + j, 4) + cs
        value = dot_nt(v[...], wbuf[cs, j]).astype(BF16)
        through[k] = value
        store = pltpu.make_async_copy(through.at[k], through_out.at[k], out_sems.at[len(stores)])
        store.start()
        stores.append(store)
        grad = value.astype(F32) + adapter_scale * jnp.dot(
            low, down_t[k], preferred_element_type=F32
        )
        return total + jnp.sum(xb[k].astype(F32) * (gain[k] * grad), axis=1, keepdims=True)

    arrived(("a2", 2))
    start_b1(2)
    over(1, 16, lambda j: low_row(j, lax.rem(my16 - j + 16, 16)).wait_recv())
    lowin[my16] = lowp[my16]
    low_sum = lowin[0]
    for k in range(1, 16):
        low_sum = low_sum + lowin[k]
    low_sum_t = low_sum.T[0:16].astype(BF16)
    part2[:, 1024:6144] = scale_factor * jnp.dot(
        low_sum_t, act[...], preferred_element_type=F32
    )
    sum2 = AdapterSum(links, part2, sums2, bufs2, sems2)
    sum2.swap()
    sum1.across()
    total = through_block(c, 0, total)
    sum2.along()
    sum_a.forward()
    sum_b.forward()
    arrived(("b1", 3))
    start_b2(3)
    arrived(("core", 0))
    total = through_block(1 - c, 0, total)
    sum1.back()

    over(1, 32, lambda j: low_out(j, lax.rem(me - j + 32, 32)).wait_recv())
    every = lax.broadcasted_iota(jnp.int32, (1024, 1), 0).astype(F32)
    pick_all = jnp.where(every == key, 1.0, 0.0).astype(BF16)
    low_slots = dot_tn(alow[...].reshape(1024, 128), pick_all).astype(BF16)
    mpart[...] = scale_factor * jnp.dot(
        low_slots[0:16], vrecv[:, c].reshape(512, 256), preferred_element_type=F32
    )
    msum = [links.send("x", k, mpart, mr.at[k - 1]) for k in (1, 2, 3)]
    sum2.across()
    arrived(("b1", 1))
    start_b2(1)
    sum1.outward()

    def into(ref):
        def put(half, span, value):
            i = span.start // 16
            ref[2 * half + i // 2, lax.rem(i, 2)] = value.astype(BF16)

        return put

    sum_a.finish(into(next_a))
    sum_c = RingSum(links, "y", next_a, relay_c, mid_c, near_c)
    sum_c.start()
    sum_b.finish(into(next_b))
    sum_d = RingSum(links, "z", next_b, relay_d, mid_d, near_d)
    sum_d.start()
    sum2.back()
    sum1.last()
    arrived(("b2", 3))
    start_core(3)
    total = through_block(c, 3, total)
    sum_c.forward()
    sum_d.forward()
    sum2.outward()
    arrived(("b1", 2))
    start_b2(2)
    arrived(("core", 3))
    total = through_block(1 - c, 3, total)
    for copy in msum:
        copy.wait_recv()
    mout[...] = (mpart[...] + mr[0]) + (mr[1] + mr[2])
    sum1.end()

    def result(ref):
        def put(half, span, value):
            ref[half] = value

        return put

    sum_c.finish(result(outa))
    sum_d.finish(result(outb))
    sum2.last()
    arrived(("b2", 1))
    start_core(1)
    total = through_block(c, 1, total)
    sum2.end()
    arrived(("core", 1))
    total = through_block(1 - c, 1, total)
    arrived(("b2", 2))
    start_core(2)
    total = through_block(c, 2, total)
    arrived(("core", 2))
    total = through_block(1 - c, 2, total)
    inverse_out[...] = inverse
    drop_out[...] = inverse * inverse * inverse * (total * (1.0 / 8192))

    for store in stores:
        store.wait()
    over(1, 8, lambda j: row(j, f).wait_send())
    over(1, 8, lambda j: back(j, f).wait_send())
    over(1, 32, lambda j: spread(j, me).wait_send())
    over(1, 32, lambda j: low_out(j, me).wait_send())
    over(1, 16, lambda j: low_row(j, my16).wait_send())
    links.finish()


def big_call(scale_factor, *args):
    dma = pltpu.SemaphoreType.DMA
    half = 2560

    def big(w):
        return [
            pltpu.VMEM((2, 64, w), BF16),
            pltpu.VMEM((2, 64, w), BF16),
            pltpu.VMEM((2, 2, 64, w), BF16),
            pltpu.VMEM((4, 2, 16, w), BF16),
        ]

    def small(w):
        return [
            pltpu.VMEM((2, 16, w), BF16),
            pltpu.VMEM((2, 16, w), BF16),
            pltpu.VMEM((2, 2, 16, w), BF16),
        ]

    def sums():
        return [
            pltpu.VMEM((8, 8192), F32),
            pltpu.VMEM((4, 8, 2048), F32),
            pltpu.VMEM((3, 8, 2048), F32),
            pltpu.VMEM((16, 8, 128), F32),
            pltpu.VMEM((16, 8, 128), F32),
            pltpu.VMEM((4, 16, 8, 128), F32),
            pltpu.VMEM((4, 16, 8, 128), F32),
        ]

    scalar = pl.BlockSpec(memory_space=pltpu.SMEM)
    shape = jax.ShapeDtypeStruct
    return pl.pallas_call(
        functools.partial(big_kernel, scale_factor),
        out_shape=(
            shape((8, 256, 1024), BF16),
            shape((256, 16), BF16),
            shape((256, 1), F32),
            shape((256, 1), F32),
            shape((2, 16, half), F32),
            shape((2, 16, half), F32),
            shape((16, 8192), F32),
            shape((16, 8192), F32),
            shape((16, 256), F32),
        ),
        in_specs=[scalar, scalar] + [VMEM] * 9 + [ANY] * 4,
        out_specs=(ANY,) + (VMEM,) * 8,
        scratch_shapes=[
            pltpu.VMEM((2, 4, 1024, 1024), BF16),
            pltpu.VMEM((8, 256, 1024), BF16),
            pltpu.VMEM((8, 256, 1024), BF16),
            pltpu.VMEM((8, 256, 1024), BF16),
            dma((96,)), dma((96,)), dma((18,)), dma((8,)),
            pltpu.VMEM((16, 1024), BF16),
            pltpu.VMEM((8, 16, 1024), BF16),
            pltpu.VMEM((8, 16, 1024), BF16),
            pltpu.VMEM((8, 16, 1024), BF16),
            pltpu.VMEM((8, 16, 1024), BF16),
            pltpu.VMEM((8, 16, 1024), BF16),
            pltpu.VMEM((8, 16, 1024), F32),
            pltpu.VMEM((4, 4, 2, 16, 256), BF16),
            pltpu.VMEM((32, 2, 16, 256), BF16),
            pltpu.VMEM((32, 128), BF16),
            pltpu.VMEM((32, 32, 128), BF16),
            pltpu.VMEM((32, 5120), BF16),
            dma((8,)), dma((8,)), dma((8,)), dma((8,)),
            dma((32,)), dma((32,)), dma((32,)), dma((32,)),
            pltpu.VMEM((2, 5120, 256), BF16),
            pltpu.VMEM((16, 256), BF16),
            pltpu.VMEM((16, 32, 128), F32),
            pltpu.VMEM((16, 32, 128), F32),
            dma((16,)), dma((16,)),
            pltpu.VMEM((512, 256), BF16),
            pltpu.VMEM((512, 256), BF16),
            pltpu.VMEM((16, 256), F32),
            pltpu.VMEM((3, 16, 256), F32),
            pltpu.VMEM((4, 2, 64, half), BF16),
            pltpu.VMEM((4, 2, 64, half), BF16),
            *big(half), *big(half), *small(half), *small(half),
            pltpu.VMEM((16, 8192), F32),
            pltpu.VMEM((16, 8192), F32),
            *sums(), *sums(),
            *[dma((16,)) for _ in range(8)],
        ],
        compiler_params=pltpu.CompilerParams(
            collective_id=0, has_side_effects=True, vmem_limit_bytes=67_043_328
        ),
        name="big",
    )(*args)


def finish_kernel(hidden, resid, through, gain, down_t, low, inverse, drop, out):
    grad = through[0].astype(F32) + adapter_scale * jnp.dot(
        low[...], down_t[0], preferred_element_type=F32
    )
    rows = (
        resid[...].astype(F32)
        + inverse[...] * (gain[0] * grad)
        - hidden[...].astype(F32) * drop[...]
    )
    out[...] = rows.astype(BF16)


def finish(hidden, resid, through, gain, down_t, low, inverse, drop):
    cols = pl.BlockSpec((256, 1024), lambda k: (0, k))

    def whole(shape):
        return pl.BlockSpec(shape, lambda k: (0, 0))

    def each(shape):
        return pl.BlockSpec((1, *shape), lambda k: (k, 0, 0))

    return pl.pallas_call(
        finish_kernel,
        grid=(8,),
        out_shape=jax.ShapeDtypeStruct((256, 8192), BF16),
        in_specs=[
            cols,
            cols,
            each((256, 1024)),
            each((1, 1024)),
            each((16, 1024)),
            whole((256, 16)),
            whole((256, 1)),
            whole((256, 1)),
        ],
        out_specs=cols,
        name="finish",
    )(hidden, resid, through, gain, down_t, low, inverse, drop)


def gelu_parts(preact):
    normal_cdf = 0.5 * (1.0 + lax.erf(preact * 0.7071067811865476))
    normal_pdf = jnp.exp(-0.5 * preact * preact) * 0.3989422804014327
    return (normal_cdf, normal_pdf)


def body(
    hidden,
    residual_gradient,
    value_output_gradient,
    attention_norm_gain,
    value_frozen_weight,
    value_down_factor,
    value_up_factor,
    merger_frozen_weight,
    merger_down_factor,
    merger_up_factor,
    merger_saved_preactivation,
    image_token_counts,
    image_encoder_owner,
    image_first_rows,
):
    scale_factor = 256.0 / (hidden.shape[0] * 128) * adapter_scale
    gain = attention_norm_gain.reshape(8, 1, 1024)
    down_t = value_down_factor.T.reshape(16, 8, 1024).transpose(1, 0, 2)
    through, low, inverse, drop, outa, outb, sums1, sums2, merger_up_gradient = big_call(
        scale_factor,
        image_first_rows,
        image_token_counts,
        image_token_counts.reshape(1, 32),
        image_encoder_owner.reshape(1, 32),
        value_output_gradient,
        value_up_factor,
        gain,
        down_t,
        merger_saved_preactivation,
        merger_down_factor.T,
        merger_up_factor,
        hidden,
        residual_gradient,
        value_frozen_weight,
        merger_frozen_weight,
    )
    layer_input_gradient = finish(
        hidden, residual_gradient, through, gain, down_t, low, inverse, drop
    )
    preact = merger_saved_preactivation.astype(F32)
    normal_cdf, normal_pdf = gelu_parts(preact)
    combined = jnp.concatenate([outa.reshape(32, 2560), outb.reshape(32, 2560)], axis=1)
    preactivation_gradient = (combined * (normal_cdf + preact * normal_pdf)).astype(BF16)
    return (
        layer_input_gradient,
        preactivation_gradient,
        sums1.T,
        sums2[:, :1024],
        sums2[:, 1024:6144].T,
        merger_up_gradient,
    )


def solution(mesh):
    tokens = P(("dp", "fsdp", "enc"), None)
    features = P(None, ("fsdp", "enc"))
    placed = (
        tokens,
        tokens,
        tokens,
        P(),
        P("fsdp", None),
        P(),
        P(),
        features,
        P(),
        features,
        tokens,
        P("dp"),
        P("dp"),
        P(("dp", "fsdp", "enc")),
    )
    return jax.shard_map(
        body,
        mesh=mesh,
        in_specs=placed,
        out_specs=(tokens, tokens, P(), P(), P(), features),
        check_vma=False,
    )
```

time: 478 us -> 131 us (0.27)
  waiting for transfers between devices: 337 us -> 0 us
  Pallas kernels: 0 us -> 124 us
  matrix products: 49.1 us -> 0 us
  other arithmetic: 27.4 us -> 1.02 us
  blocking collectives: 21.8 us -> 0 us
  between operations: 14.7 us -> 1.34 us
  local copies, waits for them, and re-layouts: 15.8 us -> 4.48 us
  starting transfers between devices: 11.3 us -> 0 us
    psum x1 -> x0, waiting for transfers between devices: 127 us -> none  [body(): lax.psum((scale_factor * down_term, scale_factor * up_term, scale_factor...]
    pallas_call x0 -> x2, Pallas kernels: none -> 124 us  [the longest x1 113 us: big_call(): pl.pallas_call(functools.partial(big_kernel, scale_factor), out_shape=(sh...]
    reduce_scatter x1 -> x0, waiting for transfers between devices: 118 us -> none  [in_one_piece(): out = lax.psum_scatter(both, axis, scatter_dimension=dim, tiled=True)]
    all_to_all x2 -> x0, waiting for transfers between devices: 54.7 us -> none  [the longest x1 46.3 us: body(): lax.all_to_all(columns, 'fsdp', split_axis=0, concat_axis=1, tiled=True)]
    dot_general x11 -> x0, matrix products: 49.1 us -> none  [the longest x1 13.4 us: body(): jnp.dot(low_part, merger_down_factor.astype(jnp.float32).T)]
    all_gather x1 -> x0, waiting for transfers between devices: 37.5 us -> none  [body(): lax.all_gather(value_output_gradient, 'fsdp', axis=0, tiled=True)]
    all_to_all x2 -> x0, blocking collectives: 21.8 us -> none  [sent_to_all(): return lax.all_to_all(copies, axis, split_axis=0, concat_axis=0, tiled=True)]
    concatenate x1 -> x0, other arithmetic: 15.5 us -> none  [in_one_piece(): both = jnp.concatenate(arrays, axis=along)]
  transfers between devices with their start and end apart: 5 -> 0, of which waited for: 5 -> 0; matrix products, arithmetic and copies ran while one was open for 3% -> 0% of each run, Pallas kernels for 0% -> 0%
where the time goes in v2:
time: 131 us
  Pallas kernels  124 us (95%)
  local copies, waits for them, and re-layouts  4.48 us (3%)
  between operations  1.34 us (1%)
    pallas_call x1, Pallas kernels, big_call(): pl.pallas_call(functools.partial(big_kernel, scale_factor), out_shape=(sh...  113 us
    pallas_call x1, Pallas kernels, finish(): pl.pallas_call(finish_kernel, grid=(8,), out_shape=jax.ShapeDtypeStruct((...  10.5 us

profile of v2, /device:TPU:1, one launch (start us, length us, event | category | flops | bytes accessed | tf_op | source)
XLA Modules:
  0.0 130.6 jit_solution(9570345816317925486)
XLA Ops:
  1.3 1.7 %copy.23 = bf16[2,8,8,1024]{3,2,0,1:T(8,128)(2,1)} copy(bf16[2,8,8,1024]{3,2,1,0:T(8,128)(2,1)} %bitcast.22) | data formatting | bytes 524288 | tf_op jit(solution)/shard_map/reshape | solution.py:808
  2.9 113.3 %big.1 = (bf16[8,256,1024]{2,1,0:T(8,128)(2,1)}, bf16[256,16]{1,0:T(8,128)(2,1)}, f32[256,1]{1,0:T(8,128)}, f32[256,1]{1,0:T(8,128)}, f32[2,16,2560]{2,1,0:T(8,1...) custom-call(s32[1]{0:T(128)S(6)} %copy.26.first_row, s32[32]{0:T(128)} %counts_s.1, ...), custom_call_target="tpu_custom_call" | custom-call | tf_op jit(solution)/shard_map/big/pallas_call | solution.py:685
  116.2 0.0 copy-start.4
  116.3 0.0 copy-start
  116.3 0.0 copy-start.2
  116.3 0.0 copy-start.3
  116.3 0.0 copy-start.1
  116.3 0.0 copy-start.5
  116.3 10.5 %finish.1 = bf16[256,8192]{1,0:T(8,128)(2,1)} custom-call(bf16[256,8192]{1,0:T(8,128)(2,1)} %hidden.3, bf16[256,8192]{1,0:T(8,128)(2,1)} %resid.3, bf16[8,256,1024]{2,1,0:T(8,128)(2,1)} %get-tuple-element.15.through, f32[8,1,1024]{2,1,0:T(1,128)} %bitcast.25, bf16[8,16,1024]{2,1,0:T(8,128)(2,1)} %bitcast.18, bf16[256,16]{1,0:T(8,128)(2,1)} %get-tuple-element.16.low, ...), custom_call_target="tpu_custom_call" | custom-call | tf_op jit(solution)/shard_map/finish/pallas_call | solution.py:765
  126.8 0.0 copy-done.4
  126.8 0.6 slice.6
  127.4 0.7 slice_bitcast_fusion
  128.2 0.0 copy-done
  128.2 0.0 copy-done.2
  128.2 0.0 copy-done.3
  128.2 1.0 fusion.7
  129.2 0.0 copy-done.1
  129.2 0.8 copy.27
  130.0 0.0 copy-done.5
  130.0 0.6 copy.28
Async XLA Ops:
  116.2 10.6 %copy-start.4 = (f32[16,8192]{1,0:T(8,128)S(1)}, f32[16,8192]{1,0:T(8,128)}, u32[]{:S(2)}) copy-start(f32[16,8192]{1,0:T(8,128)} %get-tuple-element.22) | copy-start | bytes 1572868
  116.3 11.9 %copy-start = (bf16[32,5120]{1,0:T(8,128)(2,1)S(1)}, bf16[32,5120]{1,0:T(8,128)(2,1)}, u32[]{:S(2)}) copy-start(bf16[32,5120]{1,0:T(8,128)(2,1)} %preact.1) | copy-start | bytes 983044
  116.3 11.9 %copy-start.2 = (f32[2,16,2560]{2,1,0:T(8,128)S(1)}, f32[2,16,2560]{2,1,0:T(8,128)}, u32[]{:S(2)}) copy-start(f32[2,16,2560]{2,1,0:T(8,128)} %get-tuple-element.19) | copy-start | bytes 983044
  116.3 11.9 %copy-start.3 = (f32[2,16,2560]{2,1,0:T(8,128)S(1)}, f32[2,16,2560]{2,1,0:T(8,128)}, u32[]{:S(2)}) copy-start(f32[2,16,2560]{2,1,0:T(8,128)} %get-tuple-element.20) | copy-start | bytes 983044
  116.3 12.9 %copy-start.1 = (f32[16,8192]{1,0:T(8,128)S(1)}, f32[16,8192]{1,0:T(8,128)}, u32[]{:S(2)}) copy-start(f32[16,8192]{1,0:T(8,128)} %get-tuple-element.21) | copy-start | bytes 1572868
  116.3 13.7 %copy-start.5 = (f32[16,256]{1,0:T(8,128)S(1)}, f32[16,256]{1,0:T(8,128)}, u32[]{:S(2)}) copy-start(f32[16,256]{1,0:T(8,128)} %get-tuple-element.35) | copy-start | bytes 49156

commit v3 on v2

v3 whole, which is shorter than its diff:
```python
import functools

import jax
import jax.numpy as jnp
from jax import lax
from jax.experimental import pallas as pl
from jax.experimental.pallas import tpu as pltpu
from jax.sharding import PartitionSpec as P

MAXIMG = 16
adapter_scale = 2.0
norm_eps = 1e-06
F32, BF16 = jnp.float32, jnp.bfloat16
MESH = pl.DeviceIdType.MESH
VMEM = pl.BlockSpec(memory_space=pltpu.VMEM)
ANY = pl.BlockSpec(memory_space=pl.ANY)


def dot_nt(a, b):
    return lax.dot_general(a, b, (((1,), (1,)), ((), ())), preferred_element_type=F32)


def dot_tn(a, b):
    return lax.dot_general(a, b, (((0,), (0,)), ((), ())), preferred_element_type=F32)


def wrap(v, n):
    return lax.rem(v + n, n)


def place():
    f = lax.axis_index("fsdp")
    return lax.axis_index("dp"), f // 2, lax.axis_index("enc"), lax.rem(f, 2)


class Links:
    def __init__(self, send_sems, recv_sems):
        self.x, self.y, self.z, self.c = place()
        self.send_sems, self.recv_sems = send_sems, recv_sems
        self.made = []
        self.taken = 0

    def peer(self, axis, step):
        if axis == "x":
            return {"dp": wrap(self.x + step, 4)}
        if axis == "z":
            return {"enc": wrap(self.z + step, 4)}
        if axis == "y":
            return {"fsdp": 2 * wrap(self.y + step, 4) + self.c}
        return {"fsdp": 2 * self.y + 1 - self.c}

    def take(self):
        self.taken += 1
        return self.send_sems.at[self.taken - 1], self.recv_sems.at[self.taken - 1]

    def send(self, axis, step, src, dst):
        return self.group([(axis, step, src, dst)], dst)

    def group(self, sends, whole):
        sems = self.take()
        for axis, step, src, dst in sends:
            self.copy(sems, src, dst, self.peer(axis, step)).start()
        total = self.copy(sems, whole, whole, self.peer(*sends[0][:2]))
        self.made.append(total)
        return total

    def copy(self, sems, src, dst, peer):
        return pltpu.make_async_remote_copy(
            src_ref=src,
            dst_ref=dst,
            send_sem=sems[0],
            recv_sem=sems[1],
            device_id=peer,
            device_id_type=MESH,
        )

    def finish(self):
        for copy in self.made:
            copy.wait_send()

    def meet(self, peers):
        barrier = pltpu.get_barrier_semaphore()
        for axis, step in peers:
            pl.semaphore_signal(barrier, inc=1, device_id=self.peer(axis, step), device_id_type=MESH)
        pl.semaphore_wait(barrier, len(peers))


def chunked(count, act):
    def step(i, carry):
        act(pl.ds(pl.multiple_of(i * 16, 16), 16))
        return carry

    lax.fori_loop(0, count // 16, step, 0)


class RingSum:
    def __init__(self, links, axis, blocks, relay, mid, near):
        self.links, self.axis, self.blocks = links, axis, blocks
        self.relay, self.mid, self.near = relay, mid, near
        m = links.x if axis == "x" else links.y if axis == "y" else links.z
        self.me, self.count = m, blocks.shape[2]

    def start(self):
        send, b, axis = self.links.send, self.blocks, self.axis
        far = wrap(self.me + 2, 4)
        right, left = wrap(self.me + 1, 4), wrap(self.me - 1, 4)
        self.far = [
            send(axis, 1, b.at[far, 0], self.relay.at[0]),
            send(axis, -1, b.at[far, 1], self.relay.at[1]),
        ]
        self.direct = [
            send(axis, 1, b.at[right, 1], self.near.at[0, 1]),
            send(axis, -1, b.at[left, 0], self.near.at[1, 0]),
        ]

    def forward(self):
        for way, step in ((0, 1), (1, -1)):
            self.far[way].wait_recv()
            to = wrap(self.me + step, 4)

            def add(span, way=way, to=to):
                self.mid[way, span] = (
                    self.blocks[to, way, span].astype(F32) + self.relay[way, span].astype(F32)
                ).astype(BF16)

            chunked(self.count, add)
            self.direct.append(
                self.links.send(self.axis, step, self.mid.at[way], self.near.at[way, way])
            )

    def finish(self, put):
        for copy in self.direct:
            copy.wait_recv()
        for half in range(2):

            def add(span, half=half):
                put(
                    half,
                    span,
                    self.blocks[self.me, half, span].astype(F32)
                    + self.near[0, half, span].astype(F32)
                    + self.near[1, half, span].astype(F32),
                )

            chunked(self.count, add)


class AdapterSum:
    def __init__(self, links, src, out, bufs):
        self.links, self.src, self.out = links, src, out
        self.half_in, self.ay, self.ry, self.bxz, self.rxz, self.gy, self.gc = bufs
        self.sems = links.take(), links.take()
        self.m16 = links.x * 4 + links.z
        self.other = pl.ds(pl.multiple_of((1 - links.c) * 8, 8), 8)
        self.mine = pl.ds(pl.multiple_of(links.c * 8, 8), 8)

    def plane(self, k):
        d = lax.rem(self.m16 + k, 16)
        return {"dp": d // 4, "enc": lax.rem(d, 4)}

    def spread(self, k):
        return self.links.copy(
            self.sems[0], self.bxz.at[lax.rem(self.m16 + k, 16)], self.rxz.at[k - 1], self.plane(k)
        )

    def share(self, k):
        here = self.gy.at[self.links.y, self.m16]
        return self.links.copy(self.sems[1], here, here, self.plane(k))

    def total(self, n):
        whole = self.rxz.at[0:15]
        return self.links.copy(self.sems[n], whole, whole, self.plane(1))

    def swap(self):
        self.swapped = self.links.send("c", 0, self.src.at[self.other], self.half_in)

    def along(self):
        self.swapped.wait_recv()
        for b in range(4):
            cols = slice(b * 2048, (b + 1) * 2048)
            self.ay[b] = self.src[self.mine, cols] + self.half_in[:, cols]
        y = self.links.y
        self.sent = self.links.group(
            [("y", k, self.ay.at[wrap(y + k, 4)], self.ry.at[k - 1]) for k in (1, 2, 3)], self.ry
        )

    def across(self):
        self.sent.wait_recv()
        here = self.ay.at[self.links.y]
        for b in range(16):
            cols = slice(b * 128, (b + 1) * 128)
            self.bxz[b] = (here[:, cols] + self.ry[0, :, cols]) + (
                self.ry[1, :, cols] + self.ry[2, :, cols]
            )
        over(1, 16, lambda k: self.spread(k).start())

    def back(self):
        self.total(0).wait_recv()
        value = self.bxz[self.m16]
        for k in range(15):
            value = value + self.rxz[k]
        self.gy[self.links.y, self.m16] = value
        over(1, 16, lambda k: self.share(k).start())

    def outward(self):
        self.total(1).wait_recv()
        here = self.gy.at[self.links.y]
        self.wide = self.links.group(
            [("y", k, here, here) for k in (1, 2, 3)], self.gy.at[0:3]
        )

    def last(self):
        self.wide.wait_recv()
        self.final = self.links.send("c", 0, self.gy, self.gc)
        for b in range(64):
            self.out[self.mine, b * 128 : (b + 1) * 128] = self.gy[b // 16, b % 16]

    def end(self):
        self.final.wait_recv()
        for b in range(64):
            self.out[self.other, b * 128 : (b + 1) * 128] = self.gc[b // 16, b % 16]
        self.total(0).wait_send()
        self.total(1).wait_send()


def over(lo, hi, act):
    def step(j, carry):
        act(j)
        return carry

    lax.fori_loop(lo, hi, step, 0)


def big_kernel(
    scale_factor,
    first_row, counts_s, counts, owners, up, mup,
    v_in, gain_in, down_in, preact_in, md_in, hidden, resid, wsh, wm,
    through_out, low_out_ref, inverse_out, drop_out, pgrad, sums1, sums2, mout,
    wbuf, xb, rb, through, send_sems, recv_sems, local_sems, out_sems,
    v, gain, down_t, preact, md, slope,
    vimg, xsel, rsel, vall, tout, timg, gained, visout, vrecv, actl, alow, act,
    wmb, mup_other, lowp, lowin, rows_own, rows_other, mpart, mr,
    qa, qb,
    relay_a, mid_a, near_a, next_a, relay_b, mid_b, near_b, next_b,
    relay_c, mid_c, near_c, relay_d, mid_d, near_d,
    part1, part2, *rest,
):
    bufs1, bufs2 = rest[:7], rest[7:14]
    links = Links(send_sems, recv_sems)
    x, y, z, c = links.x, links.y, links.z, links.c
    f = 2 * y + c
    me = f * 4 + z

    small = []
    pairs = ((v_in, v), (gain_in, gain), (down_in, down_t), (preact_in, preact), (md_in, md))
    for n, (src, dst) in enumerate(pairs):
        small.append(pltpu.make_async_copy(src, dst, local_sems.at[18 + n]))
        small[n].start()
    own = pltpu.make_async_copy(wsh, wbuf.at[c, 0], local_sems.at[0])
    own.start()
    loads = []
    for k in range(8):
        cols = pl.ds(k * 1024, 1024)
        a = pltpu.make_async_copy(hidden.at[:, cols], xb.at[k], local_sems.at[1 + k])
        b = pltpu.make_async_copy(resid.at[:, cols], rb.at[k], local_sems.at[9 + k])
        a.start()
        b.start()
        loads.append((a, b))
    wm_load = pltpu.make_async_copy(wm, wmb.at[0], local_sems.at[17])
    wm_load.start()

    barrier = pltpu.get_barrier_semaphore()

    def plane_peer(j):
        d = lax.rem(me + j, 32)
        return {"fsdp": d // 4, "enc": lax.rem(d, 4)}

    def greet(j):
        pl.semaphore_signal(barrier, inc=1, device_id=plane_peer(j), device_id_type=MESH)

    def greet_x(j):
        d = 4 + j
        pl.semaphore_signal(
            barrier,
            inc=1,
            device_id={"dp": lax.rem(x + d // 4, 4), "enc": lax.rem(z + d, 4)},
            device_id_type=MESH,
        )

    over(1, 32, greet)
    over(0, 12, greet_x)
    first = first_row[0]
    lane = lax.broadcasted_iota(jnp.int32, (16, 256), 1)
    line = lax.broadcasted_iota(jnp.int32, (16, 256), 0)
    sel = jnp.where(lane == line + first, 1.0, 0.0).astype(BF16)
    small[0].wait()
    vimg[...] = jnp.dot(sel, v[...], preferred_element_type=F32).astype(BF16)
    pl.semaphore_wait(barrier, 43)

    sems_row, sems_back, sems_spread = links.take(), links.take(), links.take()
    sems_low_out, sems_low_row = links.take(), links.take()
    my16 = y * 4 + z

    def row(j):
        return links.copy(sems_row, vimg, vall.at[f], {"fsdp": lax.rem(f + j, 8)})

    def back(j):
        to = lax.rem(f + j, 8)
        return links.copy(sems_back, tout.at[to], timg.at[f], {"fsdp": to})

    def spread(j):
        d = lax.rem(me + j, 32)
        return links.copy(sems_spread, visout.at[d // 8, lax.rem(d, 4)], vrecv.at[me], plane_peer(j))

    def low_out(j):
        return links.copy(sems_low_out, actl, alow.at[me], plane_peer(j))

    def low_row(j):
        d = lax.rem(my16 + j, 16)
        peer = {"fsdp": 2 * (d // 4) + c, "enc": lax.rem(d, 4)}
        return links.copy(sems_low_row, lowp.at[d], lowin.at[my16], peer)

    def all_of(sems, whole):
        return links.copy(sems, whole, whole, plane_peer(1))

    all_rows = all_of(sems_row, vall.at[0:7])
    all_back = all_of(sems_back, timg.at[0:7])
    all_spread = all_of(sems_spread, vrecv.at[0:31])
    all_low_out = all_of(sems_low_out, alow.at[0:31])
    all_low_rows = all_of(sems_low_row, lowin.at[0:15])

    def at(j, start, count):
        return wbuf.at[c, j, pl.ds(pl.multiple_of(start, 16), count)]

    def piece(step):
        return (x * 4 + wrap(z + step, 4)) * 48

    def block(step):
        return wrap(x + step, 4) * 192

    rest_at = 768
    moved = {}

    def arrived(name):
        moved[name].wait_recv()

    def group(name, rows, sends):
        moved[name] = links.group(sends, wbuf.at[c, 0, 0:rows])

    def start_y1():
        src = at(0, piece(0), 48)
        group("y1", 96, [("y", t, src, at(j, piece(0), 48)) for t, j in ((1, 3), (-1, 1))])

    def start_y2():
        sends = []
        for t, j, start, count in ((1, 3, piece(0), 32), (-1, 1, piece(0) + 32, 16)):
            sends.append(("y", t, at(j, start, count), at(2, start, count)))
        group("y2", 48, sends)

    def start_r1():
        src = at(0, rest_at, 256)
        group("r1", 512, [("y", t, src, at(j, rest_at, 256)) for t, j in ((1, 3), (-1, 1))])

    def start_r2():
        sends = []
        for t, j, start in ((1, 3, rest_at), (-1, 1, rest_at + 128)):
            sends.append(("y", t, at(j, start, 128), at(2, start, 128)))
        group("r2", 256, sends)

    def same(axis, step, j, start, count):
        here = at(j, start, count)
        return (axis, step, here, here)

    def start_a1(j):
        group(("a1", j), 96, [same("z", step, j, piece(0), 48) for step in (1, -1)])

    def start_a2(j):
        one = 32 if j == 3 else 16
        group(
            ("a2", j),
            48,
            [same("z", 1, j, piece(-1), one), same("z", -1, j, piece(1) + one, 48 - one)],
        )

    def start_b1(j):
        group(("b1", j), 384, [same("x", step, j, block(0), 192) for step in (1, -1)])

    def start_b2(j):
        group(
            ("b2", j),
            192,
            [same("x", 1, j, block(-1), 96), same("x", -1, j, block(1) + 96, 96)],
        )

    def start_core(j):
        moved["core", j] = links.send("c", 0, wbuf.at[c, j], wbuf.at[c, j])

    over(1, 8, lambda j: row(j).start())
    own.wait()
    start_y1()
    wide = links.send("c", 0, wm, wmb.at[1])
    thin = links.send("c", 0, mup, mup_other)
    start_core(0)
    vall[f] = vimg[...]

    for load in small[1:]:
        load.wait()
    low_img = dot_nt(vimg[...], up[...]).astype(BF16)
    squares_img = jnp.zeros((16, 1), F32)
    for k in range(8):
        loads[k][0].wait()
        rows = jnp.dot(sel, xb[k], preferred_element_type=F32)
        xsel[k] = rows.astype(BF16)
        squares_img = squares_img + jnp.sum(rows * rows, axis=1, keepdims=True)
    inverse_img = lax.rsqrt(squares_img * (1.0 / 8192) + norm_eps)

    all_rows.wait_recv()
    tout[...] = dot_nt(vall[...].reshape(128, 1024), wbuf[c, 0]).astype(BF16).reshape(8, 16, 1024)
    over(1, 8, lambda j: back(j).start())
    timg[f] = tout[f]
    arrived("y1")
    start_y2()
    start_a1(3)
    start_a1(1)

    for k in range(8):
        loads[k][1].wait()
        rsel[k] = jnp.dot(sel, rb[k], preferred_element_type=F32).astype(BF16)
    squares = jnp.zeros((256, 1), F32)
    for k in range(8):
        xs = xb[k].astype(F32)
        squares = squares + jnp.sum(xs * xs, axis=1, keepdims=True)
    inverse = lax.rsqrt(squares * (1.0 / 8192) + norm_eps)

    all_back.wait_recv()
    total_img = jnp.zeros((16, 1), F32)
    for k in range(8):
        grad = timg[k].astype(F32) + adapter_scale * jnp.dot(
            low_img, down_t[:, k * 1024 : (k + 1) * 1024], preferred_element_type=F32
        )
        g = gain[k] * grad
        gained[k] = g
        total_img = total_img + jnp.sum(xsel[k].astype(F32) * g, axis=1, keepdims=True)
    drop_img = inverse_img * inverse_img * inverse_img * (total_img * (1.0 / 8192))
    inside = lax.broadcasted_iota(jnp.int32, (16, 1024), 0) < counts_s[me]
    for k in range(8):
        rows = (
            rsel[k].astype(F32) + inverse_img * gained[k] - xsel[k].astype(F32) * drop_img
        )
        rows = jnp.where(inside, rows, 0.0).astype(BF16)
        for b in range(4):
            visout[k // 2, b, k % 2] = rows[:, b * 256 : (b + 1) * 256]
    over(1, 32, lambda j: spread(j).start())
    vrecv[me] = visout[y, z]
    start_r1()

    p = preact[...].astype(F32)
    normal_cdf = 0.5 * (1.0 + lax.erf(p * 0.7071067811865476))
    act[...] = (p * normal_cdf).astype(BF16)
    slope[...] = normal_cdf + p * (jnp.exp(-0.5 * p * p) * 0.3989422804014327)
    actl[...] = jnp.zeros_like(actl)
    actl[:, 0:16] = dot_nt(act[...], md[...]).astype(BF16)
    alow[me] = actl[...]

    arrived("y2")
    start_a1(2)
    arrived(("a1", 3))
    start_a2(3)
    arrived(("a1", 1))
    start_a2(1)

    low = dot_nt(v[...], up[...]).astype(BF16)
    low_out_ref[:, 0:16] = low
    low_out_ref[:, 16:128] = jnp.zeros((256, 112), BF16)
    low_t = dot_nt(up[...], v[...]).astype(BF16)
    projected_t = jnp.zeros((16, 256), F32)
    for k in range(8):
        normed = (xb[k].astype(F32) * inverse * gain[k]).astype(BF16)
        part1[:, k * 1024 : (k + 1) * 1024] = scale_factor * jnp.dot(
            low_t, normed, preferred_element_type=F32
        )
        projected_t = projected_t + dot_nt(down_t[:, k * 1024 : (k + 1) * 1024], normed)
    sum1 = AdapterSum(links, part1, sums1, bufs1)
    sum1.swap()
    part2[:, 0:1024] = scale_factor * jnp.dot(
        projected_t.astype(BF16), v[...], preferred_element_type=F32
    )
    part2[:, 6144:8192] = jnp.zeros((16, 2048), F32)

    eye = lax.broadcasted_iota(jnp.int32, (32, 32), 0) == lax.broadcasted_iota(
        jnp.int32, (32, 32), 1
    )
    earlier = lax.broadcasted_iota(jnp.int32, (32, 32), 1) < lax.broadcasted_iota(
        jnp.int32, (32, 32), 0
    )
    counts_f = counts[...].astype(F32)
    owners_f = owners[...].astype(F32)
    owner_col = jnp.sum(jnp.where(eye, owners_f, 0.0), axis=1, keepdims=True)
    count_col = jnp.sum(jnp.where(eye, counts_f, 0.0), axis=1, keepdims=True)
    start_col = jnp.sum(
        jnp.where((owner_col == owners_f) & earlier, counts_f, 0.0), axis=1, keepdims=True
    )
    slot = lax.broadcasted_iota(jnp.int32, (32, 512), 1)
    image = lax.broadcasted_iota(jnp.int32, (32, 512), 0)
    inner = (slot % 16).astype(F32)
    key = (
        jnp.sum(
            jnp.where(
                (slot // 16 == image) & (inner < count_col),
                owner_col * 32.0 + start_col + inner + 1.0,
                0.0,
            ),
            axis=0,
            keepdims=True,
        )
        - 1.0
    )

    all_spread.wait_recv()
    wide.wait_recv()
    thin.wait_recv()
    wm_load.wait()
    r = lax.broadcasted_iota(jnp.int32, (512, 1), 0)
    row_id = ((2 * (r // 128) + c) * 4 + (r // 32) % 4) * 32 + r % 32
    pick = jnp.where(row_id.astype(F32) == key, 1.0, 0.0).astype(BF16)
    rows_own[...] = jnp.dot(
        pick, vrecv[:, c].reshape(512, 256), preferred_element_type=F32
    ).astype(BF16)
    rows_other[...] = jnp.dot(
        pick, vrecv[:, 1 - c].reshape(512, 256), preferred_element_type=F32
    ).astype(BF16)
    low_part = dot_nt(rows_own[...], mup[...]) + dot_nt(rows_other[...], mup_other[...])
    lowp[...] = jnp.zeros_like(lowp)
    lowp[:, :, 0:16] = low_part.reshape(16, 32, 16)
    over(1, 16, lambda j: low_row(j).start())
    over(1, 32, lambda j: low_out(j).start())
    sum1.along()
    arrived(("a2", 3))
    start_b1(3)
    arrived(("a1", 2))
    start_a2(2)
    low_hi = low_part.astype(BF16)
    low_lo = (low_part - low_hi.astype(F32)).astype(BF16)

    def columns(n):
        cols = pl.ds(pl.multiple_of(n * 512, 512), 512)
        value = dot_nt(rows_own[...], wmb[0, cols]) + dot_nt(rows_other[...], wmb[1, cols])
        value = value + adapter_scale * (
            jnp.dot(low_hi, md[:, cols], preferred_element_type=F32)
            + jnp.dot(low_lo, md[:, cols], preferred_element_type=F32)
        )
        return value.astype(BF16)

    def fill_a(n):
        value = columns(n)
        cols = pl.ds(pl.multiple_of(n * 512, 512), 512)
        for yy in range(4):
            for zz in range(4):
                at_row = yy * 128 + zz * 32
                qa[zz, yy // 2, (yy % 2) * 32 : (yy % 2) * 32 + 32, cols] = value[
                    at_row : at_row + 32
                ]

    def fill_b(n):
        value = columns(n + 6)
        cols = pl.ds(pl.multiple_of(n * 512, 512), 512)
        qb[:, :, :, cols] = value.reshape(4, 2, 64, 512)

    sum_a = RingSum(links, "z", qa, relay_a, mid_a, near_a)
    sum_b = RingSum(links, "y", qb, relay_b, mid_b, near_b)
    over(0, 6, fill_a)
    sum_a.start()
    arrived(("a2", 1))
    start_b1(1)
    arrived("r1")
    start_r2()
    over(0, 4, fill_b)
    sum_b.start()
    arrived(("a2", 2))
    start_b1(2)

    total = jnp.zeros((256, 1), F32)
    stores = []

    def through_block(cs, j, total):
        k = 2 * lax.rem(y + j, 4) + cs
        value = dot_nt(v[...], wbuf[cs, j]).astype(BF16)
        through[k] = value
        cols = pl.ds(pl.multiple_of(k * 1024, 1024), 1024)
        store = pltpu.make_async_copy(
            through.at[k], through_out.at[:, cols], out_sems.at[len(stores)]
        )
        store.start()
        stores.append(store)
        grad = value.astype(F32) + adapter_scale * jnp.dot(
            low, down_t[:, cols], preferred_element_type=F32
        )
        return total + jnp.sum(xb[k].astype(F32) * (gain[k] * grad), axis=1, keepdims=True)

    all_low_rows.wait_recv()
    lowin[my16] = lowp[my16]
    low_sum = lowin[0]
    for k in range(1, 16):
        low_sum = low_sum + lowin[k]
    low_sum_t = low_sum.T[0:16].astype(BF16)
    part2[:, 1024:6144] = scale_factor * jnp.dot(
        low_sum_t, act[...], preferred_element_type=F32
    )
    sum2 = AdapterSum(links, part2, sums2, bufs2)
    sum2.swap()
    total = through_block(c, 0, total)
    sum2.along()
    arrived(("core", 0))
    total = through_block(1 - c, 0, total)
    sum_a.forward()
    arrived(("b1", 3))
    start_b2(3)
    sum1.across()

    all_low_out.wait_recv()
    every = lax.broadcasted_iota(jnp.int32, (1024, 1), 0).astype(F32)
    pick_all = jnp.where(every == key, 1.0, 0.0).astype(BF16)
    low_slots = dot_tn(alow[...].reshape(1024, 128), pick_all).astype(BF16)
    mpart[...] = scale_factor * jnp.dot(
        low_slots[0:16], vrecv[:, c].reshape(512, 256), preferred_element_type=F32
    )
    msum = links.group([("x", k, mpart, mr.at[k - 1]) for k in (1, 2, 3)], mr)
    sum_b.forward()
    arrived(("b1", 1))
    start_b2(1)
    def into(ref):
        def put(half, span, value):
            i = span.start // 16
            ref[2 * half + i // 2, lax.rem(i, 2)] = value.astype(BF16)

        return put

    sum_a.finish(into(next_a))
    sum_c = RingSum(links, "y", next_a, relay_c, mid_c, near_c)
    sum_c.start()
    arrived(("b1", 2))
    start_b2(2)
    sum1.back()
    sum_b.finish(into(next_b))
    sum_d = RingSum(links, "z", next_b, relay_d, mid_d, near_d)
    sum_d.start()
    sum2.across()
    arrived("r2")
    arrived(("b2", 3))
    start_core(3)
    total = through_block(c, 3, total)
    arrived(("b2", 1))
    start_core(1)
    total = through_block(c, 1, total)
    sum1.outward()
    sum2.back()
    sum_c.forward()
    sum_d.forward()
    arrived(("core", 3))
    total = through_block(1 - c, 3, total)
    arrived(("b2", 2))
    start_core(2)
    total = through_block(c, 2, total)
    sum2.outward()
    sum1.last()
    arrived(("core", 1))
    total = through_block(1 - c, 1, total)

    def result(at):
        def put(half, span, value):
            cols = slice(at, at + value.shape[1])
            rows = slice(half * 16, half * 16 + 16)
            pgrad[rows, cols] = (value * slope[rows, cols]).astype(BF16)

        return put

    sum_c.finish(result(0))
    sum_d.finish(result(next_a.shape[-1]))
    msum.wait_recv()
    mout[...] = (mpart[...] + mr[0]) + (mr[1] + mr[2])
    sum2.last()
    arrived(("core", 2))
    total = through_block(1 - c, 2, total)
    sum1.end()
    sum2.end()
    inverse_out[...] = jnp.broadcast_to(inverse, (256, 128))
    drop = inverse * inverse * inverse * (total * (1.0 / 8192))
    drop_out[...] = jnp.broadcast_to(drop, (256, 128))

    for store in stores:
        store.wait()
    for copies in (all_rows, all_back, all_spread, all_low_out, all_low_rows):
        copies.wait_send()
    links.finish()


def big_call(scale_factor, *args):
    dma = pltpu.SemaphoreType.DMA
    wide_a, wide_b = 3072, 2048

    def big(w):
        return [
            pltpu.VMEM((2, 64, w), BF16),
            pltpu.VMEM((2, 64, w), BF16),
            pltpu.VMEM((2, 2, 64, w), BF16),
            pltpu.VMEM((4, 2, 16, w), BF16),
        ]

    def small(w):
        return [
            pltpu.VMEM((2, 16, w), BF16),
            pltpu.VMEM((2, 16, w), BF16),
            pltpu.VMEM((2, 2, 16, w), BF16),
        ]

    def sums():
        return [
            pltpu.VMEM((8, 8192), F32),
            pltpu.VMEM((4, 8, 2048), F32),
            pltpu.VMEM((3, 8, 2048), F32),
            pltpu.VMEM((16, 8, 128), F32),
            pltpu.VMEM((16, 8, 128), F32),
            pltpu.VMEM((4, 16, 8, 128), F32),
            pltpu.VMEM((4, 16, 8, 128), F32),
        ]

    scalar = pl.BlockSpec(memory_space=pltpu.SMEM)
    shape = jax.ShapeDtypeStruct
    return pl.pallas_call(
        functools.partial(big_kernel, scale_factor),
        out_shape=(
            shape((256, 8192), BF16),
            shape((256, 128), BF16),
            shape((256, 128), F32),
            shape((256, 128), F32),
            shape((32, 5120), BF16),
            shape((16, 8192), F32),
            shape((16, 8192), F32),
            shape((16, 256), F32),
        ),
        in_specs=[scalar, scalar] + [VMEM] * 4 + [ANY] * 9,
        out_specs=(ANY,) + (VMEM,) * 7,
        scratch_shapes=[
            pltpu.VMEM((2, 4, 1024, 1024), BF16),
            pltpu.VMEM((8, 256, 1024), BF16),
            pltpu.VMEM((8, 256, 1024), BF16),
            pltpu.VMEM((8, 256, 1024), BF16),
            dma((64,)), dma((64,)), dma((23,)), dma((8,)),
            pltpu.VMEM((256, 1024), BF16),
            pltpu.VMEM((8, 1, 1024), F32),
            pltpu.VMEM((16, 8192), BF16),
            pltpu.VMEM((32, 5120), BF16),
            pltpu.VMEM((16, 5120), BF16),
            pltpu.VMEM((32, 5120), F32),
            pltpu.VMEM((16, 1024), BF16),
            pltpu.VMEM((8, 16, 1024), BF16),
            pltpu.VMEM((8, 16, 1024), BF16),
            pltpu.VMEM((8, 16, 1024), BF16),
            pltpu.VMEM((8, 16, 1024), BF16),
            pltpu.VMEM((8, 16, 1024), BF16),
            pltpu.VMEM((8, 16, 1024), F32),
            pltpu.VMEM((4, 4, 2, 16, 256), BF16),
            pltpu.VMEM((32, 2, 16, 256), BF16),
            pltpu.VMEM((32, 128), BF16),
            pltpu.VMEM((32, 32, 128), BF16),
            pltpu.VMEM((32, 5120), BF16),
            pltpu.VMEM((2, 5120, 256), BF16),
            pltpu.VMEM((16, 256), BF16),
            pltpu.VMEM((16, 32, 128), F32),
            pltpu.VMEM((16, 32, 128), F32),
            pltpu.VMEM((512, 256), BF16),
            pltpu.VMEM((512, 256), BF16),
            pltpu.VMEM((16, 256), F32),
            pltpu.VMEM((3, 16, 256), F32),
            pltpu.VMEM((4, 2, 64, wide_a), BF16),
            pltpu.VMEM((4, 2, 64, wide_b), BF16),
            *big(wide_a), *big(wide_b), *small(wide_a), *small(wide_b),
            pltpu.VMEM((16, 8192), F32),
            pltpu.VMEM((16, 8192), F32),
            *sums(), *sums(),
        ],
        compiler_params=pltpu.CompilerParams(
            collective_id=0, has_side_effects=True, vmem_limit_bytes=67_043_328
        ),
        name="big",
    )(*args)


def finish_kernel(
    mup, hidden, resid, through, sums1, sums2,
    gain_in, down_in, low_in, inverse_in, drop_in, pgrad_in,
    out, pgrad_out, vdown, vup, mdown, mup_out,
    hb, rb, tb, one, two, gain, down_t, low, inverse, drop, pgrad,
    load_sems, out_sems, sum_sems, small_sems,
):
    small = []
    pairs = (
        (gain_in, gain), (down_in, down_t), (low_in, low), (inverse_in, inverse),
        (drop_in, drop), (pgrad_in, pgrad),
    )
    for n, (src, dst) in enumerate(pairs):
        small.append(pltpu.make_async_copy(src, dst, small_sems.at[n]))
        small[n].start()
    loads = []

    def load(k):
        cols = pl.ds(k * 1024, 1024)
        loads.append(
            [
                pltpu.make_async_copy(src.at[:, cols], dst.at[k], load_sems.at[n, k])
                for n, (src, dst) in enumerate(((through, tb), (hidden, hb), (resid, rb)))
            ]
        )
        for copy in loads[k]:
            copy.start()

    for k in range(3):
        load(k)
    sums_in = [
        pltpu.make_async_copy(sums1, one, sum_sems.at[0]),
        pltpu.make_async_copy(sums2, two, sum_sems.at[1]),
    ]
    for copy in small:
        copy.wait()
    mup_out[...] = mup[...]
    stores = []
    for k in range(8):
        cols = slice(k * 1024, (k + 1) * 1024)
        for copy in loads[k]:
            copy.wait()
        if k < 5:
            load(k + 3)
        if k == 4:
            for copy in sums_in:
                copy.start()
        grad = tb[k].astype(F32) + adapter_scale * jnp.dot(
            low[:, 0:16], down_t[:, cols], preferred_element_type=F32
        )
        rows = (
            rb[k].astype(F32)
            + inverse[:, 0:1] * (gain[k] * grad)
            - hb[k].astype(F32) * drop[:, 0:1]
        )
        tb[k] = rows.astype(BF16)
        store = pltpu.make_async_copy(tb.at[k], out.at[:, pl.ds(k * 1024, 1024)], out_sems.at[k])
        store.start()
        stores.append(store)
    for copy in sums_in:
        copy.wait()
    stores += [
        pltpu.make_async_copy(pgrad, pgrad_out, small_sems.at[6]),
        pltpu.make_async_copy(one, vdown, sum_sems.at[2]),
        pltpu.make_async_copy(two.at[:, pl.ds(0, 1024)], vup, sum_sems.at[3]),
        pltpu.make_async_copy(two.at[:, pl.ds(1024, 5120)], mdown, sum_sems.at[4]),
    ]
    for store in stores[8:]:
        store.start()
    for store in stores:
        store.wait()


def finish(*args):
    dma = pltpu.SemaphoreType.DMA
    shape = jax.ShapeDtypeStruct
    return pl.pallas_call(
        finish_kernel,
        out_shape=(
            shape((256, 8192), BF16),
            shape((32, 5120), BF16),
            shape((16, 8192), F32),
            shape((16, 1024), F32),
            shape((16, 5120), F32),
            shape((16, 256), F32),
        ),
        in_specs=[VMEM] + [ANY] * 11,
        out_specs=(ANY, ANY, ANY, ANY, ANY, VMEM),
        scratch_shapes=[
            pltpu.VMEM((8, 256, 1024), BF16),
            pltpu.VMEM((8, 256, 1024), BF16),
            pltpu.VMEM((8, 256, 1024), BF16),
            pltpu.VMEM((16, 8192), F32),
            pltpu.VMEM((16, 8192), F32),
            pltpu.VMEM((8, 1, 1024), F32),
            pltpu.VMEM((16, 8192), BF16),
            pltpu.VMEM((256, 128), BF16),
            pltpu.VMEM((256, 128), F32),
            pltpu.VMEM((256, 128), F32),
            pltpu.VMEM((32, 5120), BF16),
            dma((3, 8)), dma((8,)), dma((5,)), dma((7,)),
        ],
        compiler_params=pltpu.CompilerParams(vmem_limit_bytes=67_043_328),
        name="finish",
    )(*args)


def body(
    hidden,
    residual_gradient,
    value_output_gradient,
    attention_norm_gain,
    value_frozen_weight,
    value_down_factor,
    value_up_factor,
    merger_frozen_weight,
    merger_down_factor,
    merger_up_factor,
    merger_saved_preactivation,
    image_token_counts,
    image_encoder_owner,
    image_first_rows,
):
    scale_factor = 256.0 / (hidden.shape[0] * 128) * adapter_scale
    gain = attention_norm_gain.reshape(8, 1, 1024)
    down_t = value_down_factor.T
    through, low, inverse, drop, pgrad, sums1, sums2, mup_sum = big_call(
        scale_factor,
        image_first_rows,
        image_token_counts,
        image_token_counts.reshape(1, 32),
        image_encoder_owner.reshape(1, 32),
        value_up_factor,
        merger_up_factor,
        value_output_gradient,
        gain,
        down_t,
        merger_saved_preactivation,
        merger_down_factor.T,
        hidden,
        residual_gradient,
        value_frozen_weight,
        merger_frozen_weight,
    )
    layer_input_gradient, preactivation_gradient, vdown, vup, mdown, merger_up_gradient = finish(
        mup_sum,
        hidden,
        residual_gradient,
        through,
        sums1,
        sums2,
        gain,
        down_t,
        low,
        inverse,
        drop,
        pgrad,
    )
    return (
        layer_input_gradient,
        preactivation_gradient,
        vdown.T,
        vup,
        mdown.T,
        merger_up_gradient,
    )


def solution(mesh):
    tokens = P(("dp", "fsdp", "enc"), None)
    features = P(None, ("fsdp", "enc"))
    placed = (
        tokens,
        tokens,
        tokens,
        P(),
        P("fsdp", None),
        P(),
        P(),
        features,
        P(),
        features,
        tokens,
        P("dp"),
        P("dp"),
        P(("dp", "fsdp", "enc")),
    )
    return jax.shard_map(
        body,
        mesh=mesh,
        in_specs=placed,
        out_specs=(tokens, tokens, P(), P(), P(), features),
        check_vma=False,
    )
```

time: 131 us -> 108 us (0.82)
  Pallas kernels: 124 us -> 107 us
  local copies, waits for them, and re-layouts: 4.48 us -> 0 us
    pallas_call x1, Pallas kernels: 113 us -> 96.3 us  [big_call(): pl.pallas_call(functools.partial(big_kernel, scale_factor), out_shape=(sh...]
    reshape x1 -> x0, local copies, waits for them, and re-layouts: 1.67 us -> none  [body(): down_t = value_down_factor.T.reshape(16, 8, 1024).transpose(1, 0, 2)]
    unnamed x14 -> x0, local copies, waits for them, and re-layouts: 1.43 us -> none
where the time goes in v3:
time: 108 us
  Pallas kernels  107 us (99%)
  between operations  1.45 us (1%)
    pallas_call x1, Pallas kernels, big_call(): pl.pallas_call(functools.partial(big_kernel, scale_factor), out_shape=(sh...  96.3 us
    pallas_call x1, Pallas kernels, finish(): pl.pallas_call(finish_kernel, out_shape=(shape((256, 8192), BF16), shape(...  10.2 us

profile of v3, /device:TPU:1, one launch (start us, length us, event | category | flops | bytes accessed | tf_op | source)
XLA Modules:
  0.0 108.0 jit_solution(2353532414014310116)
XLA Ops:
  1.3 96.3 %big.1 = (bf16[256,8192]{1,0:T(8,128)(2,1)}, bf16[256,128]{1,0:T(8,128)(2,1)}, f32[256,128]{1,0:T(8,128)}, f32[256,128]{1,0:T(8,128)}, bf16[32,5120]{1,0:T(8,128...) custom-call(s32[1]{0:T(128)S(6)} %copy.20.first_row, s32[32]{0:T(128)} %counts_s.1, ...), custom_call_target="tpu_custom_call" | custom-call | tf_op jit(solution)/shard_map/big/pallas_call | solution.py:729
  97.6 10.2 %finish.1 = (bf16[256,8192]{1,0:T(8,128)(2,1)}, bf16[32,5120]{1,0:T(8,128)(2,1)}, f32[16,8192]{1,0:T(8,128)}, f32[16,1024]{1,0:T(8,128)}, f32[16,5120]{1,0:T(8,128)}, /*index=5*/f32[16,256]{1,0:T(8,128)}) custom-call(f32[16,256]{1,0:T(8,128)} %get-tuple-element.20.mup, bf16[256,8192]{1,0:T(8,128)(2,1)} %hidden.3, bf16[256,8192]{1,0:T(8,128)(2,1)} %resid.3, ...), custom_call_target="tpu_custom_call" | custom-call | tf_op jit(solution)/shard_map/finish/pallas_call | solution.py:865

commit v4 on v3

--- a/solution.py
+++ b/solution.py
@@ -338,7 +338,9 @@
     def block(step):
         return wrap(x + step, 4) * 192
 
-    rest_at = 768
+    def early(step):
+        return 768 + wrap(x + step, 4) * 64
+
     moved = {}
 
     def arrived(name):
@@ -358,14 +360,24 @@
         group("y2", 48, sends)
 
     def start_r1():
-        src = at(0, rest_at, 256)
-        group("r1", 512, [("y", t, src, at(j, rest_at, 256)) for t, j in ((1, 3), (-1, 1))])
+        src = at(0, early(0), 64)
+        group("r1", 128, [("y", t, src, at(j, early(0), 64)) for t, j in ((1, 3), (-1, 1))])
 
     def start_r2():
         sends = []
-        for t, j, start in ((1, 3, rest_at), (-1, 1, rest_at + 128)):
-            sends.append(("y", t, at(j, start, 128), at(2, start, 128)))
-        group("r2", 256, sends)
+        for t, j, start in ((1, 3, early(0)), (-1, 1, early(0) + 32)):
+            sends.append(("y", t, at(j, start, 32), at(2, start, 32)))
+        group("r2", 64, sends)
+
+    def start_c1(j):
+        group(("c1", j), 128, [same("x", step, j, early(0), 64) for step in (1, -1)])
+
+    def start_c2(j):
+        group(
+            ("c2", j),
+            64,
+            [same("x", 1, j, early(-1), 32), same("x", -1, j, early(1) + 32, 32)],
+        )
 
     def same(axis, step, j, start, count):
         here = at(j, start, count)
@@ -393,11 +405,14 @@
         )
 
     def start_core(j):
+        if j:
+            arrived(("c2", j))
         moved["core", j] = links.send("c", 0, wbuf.at[c, j], wbuf.at[c, j])
 
     over(1, 8, lambda j: row(j).start())
     own.wait()
     start_y1()
+    start_r1()
     wide = links.send("c", 0, wm, wmb.at[1])
     thin = links.send("c", 0, mup, mup_other)
     start_core(0)
@@ -422,6 +437,10 @@
     start_y2()
     start_a1(3)
     start_a1(1)
+    arrived("r1")
+    start_r2()
+    start_c1(3)
+    start_c1(1)
 
     for k in range(8):
         loads[k][1].wait()
@@ -452,7 +471,6 @@
             visout[k // 2, b, k % 2] = rows[:, b * 256 : (b + 1) * 256]
     over(1, 32, lambda j: spread(j).start())
     vrecv[me] = visout[y, z]
-    start_r1()
 
     p = preact[...].astype(F32)
     normal_cdf = 0.5 * (1.0 + lax.erf(p * 0.7071067811865476))
@@ -464,6 +482,12 @@
 
     arrived("y2")
     start_a1(2)
+    arrived("r2")
+    start_c1(2)
+    arrived(("c1", 3))
+    start_c2(3)
+    arrived(("c1", 1))
+    start_c2(1)
     arrived(("a1", 3))
     start_a2(3)
     arrived(("a1", 1))
@@ -539,6 +563,8 @@
     start_b1(3)
     arrived(("a1", 2))
     start_a2(2)
+    arrived(("c1", 2))
+    start_c2(2)
     low_hi = low_part.astype(BF16)
     low_lo = (low_part - low_hi.astype(F32)).astype(BF16)
 
@@ -562,20 +588,19 @@
                 ]
 
     def fill_b(n):
-        value = columns(n + 6)
+        value = columns(n + 5)
         cols = pl.ds(pl.multiple_of(n * 512, 512), 512)
         qb[:, :, :, cols] = value.reshape(4, 2, 64, 512)
 
     sum_a = RingSum(links, "z", qa, relay_a, mid_a, near_a)
     sum_b = RingSum(links, "y", qb, relay_b, mid_b, near_b)
-    over(0, 6, fill_a)
+    over(0, 5, fill_a)
     sum_a.start()
     arrived(("a2", 1))
     start_b1(1)
-    arrived("r1")
-    start_r2()
-    over(0, 4, fill_b)
+    over(0, 5, fill_b)
     sum_b.start()
+    sum1.across()
     arrived(("a2", 2))
     start_b1(2)
 
@@ -615,7 +640,6 @@
     sum_a.forward()
     arrived(("b1", 3))
     start_b2(3)
-    sum1.across()
 
     all_low_out.wait_recv()
     every = lax.broadcasted_iota(jnp.int32, (1024, 1), 0).astype(F32)
@@ -635,25 +659,22 @@
 
         return put
 
+    sum1.back()
     sum_a.finish(into(next_a))
     sum_c = RingSum(links, "y", next_a, relay_c, mid_c, near_c)
     sum_c.start()
     arrived(("b1", 2))
     start_b2(2)
-    sum1.back()
     sum_b.finish(into(next_b))
     sum_d = RingSum(links, "z", next_b, relay_d, mid_d, near_d)
     sum_d.start()
     sum2.across()
-    arrived("r2")
     arrived(("b2", 3))
     start_core(3)
     total = through_block(c, 3, total)
     arrived(("b2", 1))
     start_core(1)
     total = through_block(c, 1, total)
-    sum1.outward()
-    sum2.back()
     sum_c.forward()
     sum_d.forward()
     arrived(("core", 3))
@@ -661,10 +682,10 @@
     arrived(("b2", 2))
     start_core(2)
     total = through_block(c, 2, total)
-    sum2.outward()
-    sum1.last()
     arrived(("core", 1))
     total = through_block(1 - c, 1, total)
+    sum1.outward()
+    sum2.back()
 
     def result(at):
         def put(half, span, value):
@@ -678,9 +699,11 @@
     sum_d.finish(result(next_a.shape[-1]))
     msum.wait_recv()
     mout[...] = (mpart[...] + mr[0]) + (mr[1] + mr[2])
-    sum2.last()
     arrived(("core", 2))
     total = through_block(1 - c, 2, total)
+    sum2.outward()
+    sum1.last()
+    sum2.last()
     sum1.end()
     sum2.end()
     inverse_out[...] = jnp.broadcast_to(inverse, (256, 128))
@@ -696,7 +719,7 @@
 
 def big_call(scale_factor, *args):
     dma = pltpu.SemaphoreType.DMA
-    wide_a, wide_b = 3072, 2048
+    wide_a, wide_b = 2560, 2560
 
     def big(w):
         return [
@@ -745,7 +768,7 @@
             pltpu.VMEM((8, 256, 1024), BF16),
             pltpu.VMEM((8, 256, 1024), BF16),
             pltpu.VMEM((8, 256, 1024), BF16),
-            dma((64,)), dma((64,)), dma((23,)), dma((8,)),
+            dma((70,)), dma((70,)), dma((23,)), dma((8,)),
             pltpu.VMEM((256, 1024), BF16),
             pltpu.VMEM((8, 1, 1024), F32),
             pltpu.VMEM((16, 8192), BF16),

time: 108 us -> 108 us (level)
  no operation moved by 1% of the time
where the time goes in v4:
time: 108 us
  Pallas kernels  107 us (99%)
  between operations  1.45 us (1%)
    pallas_call x1, Pallas kernels, big_call(): pl.pallas_call(functools.partial(big_kernel, scale_factor), out_shape=(sh...  96.3 us
    pallas_call x1, Pallas kernels, finish(): pl.pallas_call(finish_kernel, out_shape=(shape((256, 8192), BF16), shape(...  10.2 us

profile of v4, /device:TPU:1, one launch (start us, length us, event | category | flops | bytes accessed | tf_op | source)
XLA Modules:
  0.0 108.0 jit_solution(4638416035641421470)
XLA Ops:
  1.3 96.3 %big.1 = (bf16[256,8192]{1,0:T(8,128)(2,1)}, bf16[256,128]{1,0:T(8,128)(2,1)}, f32[256,128]{1,0:T(8,128)}, f32[256,128]{1,0:T(8,128)}, bf16[32,5120]{1,0:T(8,128...) custom-call(s32[1]{0:T(128)S(6)} %copy.20.first_row, s32[32]{0:T(128)} %counts_s.1, ...), custom_call_target="tpu_custom_call" | custom-call | tf_op jit(solution)/shard_map/big/pallas_call | solution.py:752
  97.6 10.2 %finish.1 = (bf16[256,8192]{1,0:T(8,128)(2,1)}, bf16[32,5120]{1,0:T(8,128)(2,1)}, f32[16,8192]{1,0:T(8,128)}, f32[16,1024]{1,0:T(8,128)}, f32[16,5120]{1,0:T(8,128)}, /*index=5*/f32[16,256]{1,0:T(8,128)}) custom-call(f32[16,256]{1,0:T(8,128)} %get-tuple-element.20.mup, bf16[256,8192]{1,0:T(8,128)(2,1)} %hidden.3, bf16[256,8192]{1,0:T(8,128)(2,1)} %resid.3, ...), custom_call_target="tpu_custom_call" | custom-call | tf_op jit(solution)/shard_map/finish/pallas_call | solution.py:888

commit v5 on v4

--- a/solution.py
+++ b/solution.py
@@ -674,6 +674,7 @@
     total = through_block(c, 3, total)
     arrived(("b2", 1))
     start_core(1)
+    sum2.back()
     total = through_block(c, 1, total)
     sum_c.forward()
     sum_d.forward()
@@ -682,10 +683,10 @@
     arrived(("b2", 2))
     start_core(2)
     total = through_block(c, 2, total)
+    sum2.outward()
+    sum1.outward()
     arrived(("core", 1))
     total = through_block(1 - c, 1, total)
-    sum1.outward()
-    sum2.back()
 
     def result(at):
         def put(half, span, value):
@@ -701,7 +702,6 @@
     mout[...] = (mpart[...] + mr[0]) + (mr[1] + mr[2])
     arrived(("core", 2))
     total = through_block(1 - c, 2, total)
-    sum2.outward()
     sum1.last()
     sum2.last()
     sum1.end()

time: 108 us -> 111 us (1.028)
  Pallas kernels: 107 us -> 109 us
    pallas_call x1, Pallas kernels: 96.3 us -> 98.6 us  [big_call(): pl.pallas_call(functools.partial(big_kernel, scale_factor), out_shape=(sh...]
where the time goes in v5:
time: 111 us; the launch traced here: 110 us
  Pallas kernels  109 us (98%)
  between operations  1.45 us (1%)
    pallas_call x1, Pallas kernels, big_call(): pl.pallas_call(functools.partial(big_kernel, scale_factor), out_shape=(sh...  98.6 us
    pallas_call x1, Pallas kernels, finish(): pl.pallas_call(finish_kernel, out_shape=(shape((256, 8192), BF16), shape(...  10.2 us

profile of v5, /device:TPU:1, one launch (start us, length us, event | category | flops | bytes accessed | tf_op | source)
XLA Modules:
  0.0 110.3 jit_solution(14464960321502217031)
XLA Ops:
  1.3 98.6 %big.1 = (bf16[256,8192]{1,0:T(8,128)(2,1)}, bf16[256,128]{1,0:T(8,128)(2,1)}, f32[256,128]{1,0:T(8,128)}, f32[256,128]{1,0:T(8,128)}, bf16[32,5120]{1,0:T(8,128...) custom-call(s32[1]{0:T(128)S(6)} %copy.20.first_row, s32[32]{0:T(128)} %counts_s.1, ...), custom_call_target="tpu_custom_call" | custom-call | tf_op jit(solution)/shard_map/big/pallas_call | solution.py:752
  99.9 10.2 %finish.1 = (bf16[256,8192]{1,0:T(8,128)(2,1)}, bf16[32,5120]{1,0:T(8,128)(2,1)}, f32[16,8192]{1,0:T(8,128)}, f32[16,1024]{1,0:T(8,128)}, f32[16,5120]{1,0:T(8,128)}, /*index=5*/f32[16,256]{1,0:T(8,128)}) custom-call(f32[16,256]{1,0:T(8,128)} %get-tuple-element.20.mup, bf16[256,8192]{1,0:T(8,128)(2,1)} %hidden.3, bf16[256,8192]{1,0:T(8,128)(2,1)} %resid.3, ...), custom_call_target="tpu_custom_call" | custom-call | tf_op jit(solution)/shard_map/finish/pallas_call | solution.py:888
